TPU v7x, 32 devices: a whole 2x2x4 slice. The times are simulated.
32 devices in a mesh: kgrp: 2 (over y), band: 4 (over z), fft: 4 (over x, core).
Axes of the slice: x: 2, y: 2, z: 4, core: 2. Of those that a mesh axis runs over, the one named last changes fastest.
Arguments:
- orbitals: float32 [8, 64, 64, 128], P(('kgrp', 'band'), 'fft'), parts along dimension 0, may hold values from -6 to 6
- partners: float32 [8, 64, 64, 128], P(('kgrp', 'band'), 'fft'), parts along dimension 0, may hold values from -6 to 6
- shift_table: float32 [8, 3], replicated, may hold values from -0.5 to 0.5
- shift_index: int32 [8], P('kgrp'), parts along dimension 0, may hold values from 0 to 7
Outputs:
- potential: float32 [8, 64, 64, 128], P(('kgrp', 'band'), 'fft'), parts along dimension 0
- projector: float32 [8, 64, 64, 128], P(('kgrp', 'band'), 'fft'), parts along dimension 0
There are 2 independent parts, one for each index of `kgrp`. A program takes and returns all parts, laid end to end along the dimension named above; an argument that names none is the same for every part. Nothing has to cross between parts.
All inputs are finite; a program needn't handle non-finite values.
Results may differ from a plain program's by a relative error of at most 0.0001.
Values sent between devices are 32-bit elements; how exact they have to be, the bound alone decides.
A program may use at most 64 MiB of HBM per device.

v0:
```python
import math

import jax
import jax.numpy as jnp
from jax import lax
from jax.sharding import PartitionSpec as P

HIGHEST = lax.Precision.HIGHEST
SCREEN_SQUARE = 0.25
FOUR_PI = 4.0 * math.pi


def angle_pair(extent, sign):
    positions = jnp.arange(extent, dtype=jnp.int32)
    product = positions[:, None] * positions[None, :] % extent
    angle = 2.0 * math.pi / extent * product.astype(jnp.float32)
    return (jnp.cos(angle), sign * jnp.sin(angle))


def last_table(extent, sign):
    cosine, sine = angle_pair(extent, sign)
    upper = jnp.concatenate([cosine, sine], axis=1)
    lower = jnp.concatenate([-sine, cosine], axis=1)
    return jnp.concatenate([upper, lower], axis=0)


def middle_table(extent, sign):
    cosine, sine = angle_pair(extent, sign)
    return jnp.stack([jnp.stack([cosine, -sine], -1), jnp.stack([sine, cosine], -1)], 1)


def along_last(field, table):
    shape = field.shape
    flat = field.reshape(-1, shape[-1])
    return jnp.dot(flat, table, precision=HIGHEST).reshape(shape)


def along_axis(field, table, axis_number):
    shape = field.shape
    extent = shape[-1] // 2
    split = field.reshape(shape[0], shape[1], shape[2], 2, extent)
    if axis_number == 1:
        result = jnp.einsum("kcnd,pnbdz->pkbcz", table, split, precision=HIGHEST)
    else:
        result = jnp.einsum("kcnd,pandz->pakcz", table, split, precision=HIGHEST)
    return result.reshape(shape)


def times_conj(left, right):
    extent = left.shape[-1] // 2
    left_real, left_imag = (left[..., :extent], left[..., extent:])
    right_real, right_imag = (right[..., :extent], right[..., extent:])
    return jnp.concatenate(
        [
            left_real * right_real + left_imag * right_imag,
            left_real * right_imag - left_imag * right_real,
        ],
        axis=-1,
    )


def times(left, right):
    extent = left.shape[-1] // 2
    left_real, left_imag = (left[..., :extent], left[..., extent:])
    right_real, right_imag = (right[..., :extent], right[..., extent:])
    return jnp.concatenate(
        [
            left_real * right_real - left_imag * right_imag,
            left_real * right_imag + left_imag * right_real,
        ],
        axis=-1,
    )


def rotate(field):
    extent = field.shape[-1] // 2
    return jnp.concatenate([field[..., extent:], -field[..., :extent]], axis=-1)


def frequency(positions, extent):
    return jnp.where(positions < extent // 2, positions, positions - extent).astype(jnp.float32)


def kernel_block(qvectors, y_count, extent):
    first_freq = frequency(jnp.arange(extent, dtype=jnp.int32), extent)
    second_freq = frequency(jnp.arange(y_count, dtype=jnp.int32), extent)
    third_freq = frequency(jnp.arange(2 * extent, dtype=jnp.int32) % extent, extent)
    first_part = (first_freq[None, :] + qvectors[:, 0:1]) ** 2
    second_part = (second_freq[None, :] + qvectors[:, 1:2]) ** 2
    third_part = (third_freq[None, :] + qvectors[:, 2:3]) ** 2
    denominator = (
        first_part[:, :, None, None]
        + second_part[:, None, :, None]
        + third_part[:, None, None, :]
        + SCREEN_SQUARE
    )
    return FOUR_PI / extent**3 / denominator


def shifts_for(shift_table, shift_index, start_at, length):
    picked = lax.dynamic_slice_in_dim(shift_index, start_at, length)
    onehot = (picked[:, None] == jnp.arange(shift_table.shape[0], dtype=jnp.int32)[None, :]).astype(
        jnp.float32
    )
    return jnp.dot(onehot, shift_table, precision=HIGHEST)


def factor_inverse(over_real, over_imag):
    matrix_order = over_real.shape[0]
    positions = jnp.arange(matrix_order, dtype=jnp.int32)
    zero_start = jnp.zeros_like(over_real)

    def chol_step(column, lowers):
        lower_real, lower_imag = lowers
        row_real = lower_real[column]
        row_imag = lower_imag[column]
        resid_real = over_real[:, column] - (
            jnp.dot(lower_real, row_real, precision=HIGHEST)
            + jnp.dot(lower_imag, row_imag, precision=HIGHEST)
        )
        resid_imag = over_imag[:, column] - (
            jnp.dot(lower_imag, row_real, precision=HIGHEST)
            - jnp.dot(lower_real, row_imag, precision=HIGHEST)
        )
        pivot_value = jnp.sqrt(resid_real[column])
        below_diag = positions > column
        at_diag = positions == column
        new_real = jnp.where(
            below_diag, resid_real / pivot_value, jnp.where(at_diag, pivot_value, 0.0)
        )
        new_imag = jnp.where(below_diag, resid_imag / pivot_value, 0.0)
        chosen = positions[None, :] == column
        return (
            jnp.where(chosen, new_real[:, None], lower_real),
            jnp.where(chosen, new_imag[:, None], lower_imag),
        )

    lower_real, lower_imag = lax.fori_loop(0, matrix_order, chol_step, (zero_start, zero_start))

    def solve_step(row_index, inverses):
        inv_real, inv_imag = inverses
        row_real = lower_real[row_index]
        row_imag = lower_imag[row_index]
        sum_real = jnp.dot(row_real, inv_real, precision=HIGHEST) - jnp.dot(
            row_imag, inv_imag, precision=HIGHEST
        )
        sum_imag = jnp.dot(row_real, inv_imag, precision=HIGHEST) + jnp.dot(
            row_imag, inv_real, precision=HIGHEST
        )
        unit_row = (positions == row_index).astype(over_real.dtype)
        pivot_value = lower_real[row_index, row_index]
        new_real = (unit_row - sum_real) / pivot_value
        new_imag = -sum_imag / pivot_value
        chosen = positions[:, None] == row_index
        return (
            jnp.where(chosen, new_real[None, :], inv_real),
            jnp.where(chosen, new_imag[None, :], inv_imag),
        )

    return lax.fori_loop(0, matrix_order, solve_step, (zero_start, zero_start))


def body(orbitals, partners, shift_table, shift_index):
    extent = orbitals.shape[2]
    band_count = orbitals.shape[0]
    tables = (
        last_table(extent, -1.0),
        middle_table(extent, -1.0),
        last_table(extent, 1.0),
        middle_table(extent, 1.0),
    )
    my_band = lax.axis_index("band")
    forward_last, forward_mid, inverse_last, inverse_mid = tables
    full_orbitals = lax.all_gather(orbitals, "fft", axis=1, tiled=True)
    every_slab = lax.all_gather(partners, "band", axis=0, tiled=True)
    own_grids = lax.all_to_all(every_slab, "fft", split_axis=0, concat_axis=1, tiled=True)
    own_count = own_grids.shape[0]
    qvectors = shifts_for(shift_table, shift_index, lax.axis_index("fft") * own_count, own_count)

    def one_partner(member, running):
        single = lax.dynamic_slice_in_dim(own_grids, member, 1, 0)
        kernel = kernel_block(lax.dynamic_slice_in_dim(qvectors, member, 1, 0), extent, extent)
        density = times_conj(single, full_orbitals)
        spectrum = (
            along_axis(
                along_axis(along_last(density, forward_last), forward_mid, 2), forward_mid, 1
            )
            * kernel
        )
        field = along_last(
            along_axis(along_axis(spectrum, inverse_mid, 1), inverse_mid, 2), inverse_last
        )
        return running + times(single, field)

    partial_value = lax.fori_loop(
        0, own_count, one_partner, jnp.zeros(full_orbitals.shape, jnp.float32)
    )
    potential = lax.psum_scatter(partial_value, "fft", scatter_dimension=1, tiled=True)
    every_pot = lax.all_gather(potential, "band", axis=0, tiled=True)
    turned = rotate(every_pot)
    total_bands = every_pot.shape[0]
    flat_orbitals = orbitals.reshape(band_count, -1)
    flat_pot = every_pot.reshape(total_bands, -1)
    flat_turned = turned.reshape(total_bands, -1)
    volume = float(extent**3)
    rows_real = jnp.einsum("ik,jk->ij", flat_orbitals, flat_pot, precision=HIGHEST) / volume
    rows_imag = jnp.einsum("ik,jk->ij", flat_orbitals, flat_turned, precision=HIGHEST) / volume
    start_row = my_band * band_count
    summed_real, summed_imag = lax.psum((rows_real, rows_imag), "fft")
    over_real, over_imag = (
        lax.all_gather(summed_real, "band", axis=0, tiled=True),
        lax.all_gather(summed_imag, "band", axis=0, tiled=True),
    )
    inv_real, inv_imag = factor_inverse(over_real, over_imag)
    coef_real = lax.dynamic_slice_in_dim(inv_real, start_row, band_count, 0)
    coef_imag = lax.dynamic_slice_in_dim(inv_imag, start_row, band_count, 0)
    projector = jnp.dot(coef_real, flat_pot, precision=HIGHEST) + jnp.dot(
        coef_imag, flat_turned, precision=HIGHEST
    )
    return (potential, projector.reshape(orbitals.shape))


def solution(mesh):
    in_specs = (
        P(("kgrp", "band"), "fft", None, None),
        P(("kgrp", "band"), "fft", None, None),
        P(),
        P("kgrp"),
    )
    out_specs = (P(("kgrp", "band"), "fft", None, None), P(("kgrp", "band"), "fft", None, None))
    return jax.shard_map(body, mesh=mesh, in_specs=in_specs, out_specs=out_specs, check_vma=False)
```

profile of v0, /device:TPU:0, one launch (start us, length us, event | category | flops | bytes accessed | tf_op | source)
XLA Modules:
  0.0 318.6 jit_solution(13090244418852395720)
XLA Ops:
  7.2 0.7 all-gather.6.cloned.1.call-update
  8.0 0.7 all-gather.8.cloned.1.call-update
  8.8 49.1 %all-gather.6.cloned.1.call-done = f32[4,16,64,128]{3,2,1,0:T(8,128)} async-done(((f32[1,16,64,128]{3,2,1,0:T(8,128)}), f32[4,16,64,128]{3,2,1,0:T(8,128)}) %all-gather.6.cloned.1.call-update) | async-done | bytes 2097168 | tf_op jit(solution)/shard_map/all_gather | solution.py:175
  58.0 3.6 %all-to-all-start = ((f32[4,16,64,128]{3,2,1,0:T(8,128)}), f32[4,16,64,128]{3,2,1,0:T(8,128)S(1)}, u32[]{:S(2)}, u32[]{:S(2)}) async-start(f32[4,16,64,128]{3,2,1,0:T(8,128)} %all-gather.6.cloned.1.call-done), calls=%async_computation | async-start | bytes 4194304 | tf_op jit(solution)/shard_map/all_to_all | solution.py:176
  62.6 0.8 fusion.127
  64.5 1.3 add_multiply_fusion
  66.5 25.8 %all-gather.8.cloned.1.call-done = f32[1,64,64,128]{3,2,0,1:T(8,128)} async-done(((f32[1,16,64,128]{3,2,0,1:T(8,128)}), f32[1,64,64,128]{3,2,0,1:T(8,128)}) %all-gather.8.cloned.1.call-update) | async-done | bytes 2097168 | tf_op jit(solution)/shard_map/all_gather | solution.py:174
  92.3 6.2 %all-to-all-done = f32[4,16,64,128]{3,2,1,0:T(8,128)S(1)} async-done(((f32[4,16,64,128]{3,2,1,0:T(8,128)}), f32[4,16,64,128]{3,2,1,0:T(8,128)S(1)}, u32[]{:S(2)}, u32[]{:S(2)}) %all-to-all-start) | async-done | bytes 2097184 | tf_op jit(solution)/shard_map/all_to_all | solution.py:176
  98.5 3.6 %multiply_add_fusion.1 = (f32[1,64,64,64]{3,2,1,0:T(8,128)S(1)}, f32[1,64,64,64]{3,2,1,0:T(8,128)S(1)}) fusion(f32[1,64,64,128]{3,2,1,0:T(8,128)} %bitcast.298, f32[1,64,64,128]{3,2,1,0:T(8,128)S(1)} %bitcast.293), kind=kLoop, calls=%fused_computation.93 | loop fusion | flops 1572864 | bytes 6291456 | tf_op jit(solution)/shard_map/while/body/eval_jaxpr/add | solution.py:55
  102.1 6.6 %fusion.65 = f32[64,64,2,64]{1,3,2,0:T(8,128)S(1)} fusion(f32[2,64,128,1]{2,1,0,3:T(8,128)S(1)} %bitcast.307, f32[1,64,64,64]{3,2,1,0:T(8,128)S(1)} %get-tuple-element.361, f32[1,64,64,64]{3,2,1,0:T(8,128)S(1)} %get-tuple-element.360), kind=kOutput, calls=%fused_computation.81 | convolution fusion | flops 805830656 | bytes 4259840 | tf_op jit(solution)/shard_map/while/body/eval_jaxpr/dot_general | solution.py:35
  108.7 5.5 %fusion.51 = f32[64,64,2,64,1]{1,3,2,0,4:T(8,128)} fusion(f32[64,64,2,64]{1,3,2,0:T(8,128)S(1)} %fusion.65, f32[64,1,64,2]{2,0,3,1:T(8,128)S(1)} %get-tuple-element.366, f32[64,1,64,2]{2,0,3,1:T(8,128)S(1)} %get-tuple-element.367), kind=kOutput, calls=%fused_computation.69 | convolution fusion | flops 805322752 | bytes 4259840 | tf_op jit(solution)/shard_map/while/body/eval_jaxpr/kcnd,pandz->pakcz/dot_general | solution.py:45
  114.2 6.1 %copy.31 = f32[64,64,2,64,1]{0,3,2,4,1:T(8,128)} copy(f32[64,64,2,64,1]{1,3,2,0,4:T(8,128)} %fusion.51) | data formatting | bytes 4194304 | tf_op jit(solution)/shard_map/reshape.21
  120.3 5.8 %fusion.95 = f32[64,64,64,2,1]{2,1,4,3,0:T(8,128)S(1)} fusion(f32[64,64,2,64,1]{0,3,2,4,1:T(8,128)} %copy.31, f32[64,1,64,2]{2,0,3,1:T(8,128)S(1)} %get-tuple-element.366, f32[64,1,64,2]{2,0,3,1:T(8,128)S(1)} %get-tuple-element.367), kind=kOutput, calls=%fused_computation.108 | convolution fusion | flops 805322752 | bytes 4259840 | tf_op jit(solution)/shard_map/while/body/eval_jaxpr/kcnd,pnbdz->pkbcz/dot_general | solution.py:43
  126.1 5.5 %fusion.54 = f32[64,64,2,64,1]{0,3,2,1,4:T(8,128)} fusion(f32[64,64,64,2,1]{2,1,4,3,0:T(8,128)S(1)} %fusion.95, f32[2,64]{1,0:T(2,128)S(1)} %fusion.132, f32[64,64]{0,1:T(8,128)S(1)} %broadcast_add_fusion, f32[64,1,64,2]{2,0,3,1:T(8,128)S(1)} %get-tuple-element.365, f32[64,1,64,2]{2,0,3,1:T(8,128)S(1)} %get-tuple-element.364), kind=kOutput, calls=%fused_computation.70 | convolution fusion | flops 807419904 | bytes 4276736 | tf_op jit(solution)/shard_map/while/body/eval_jaxpr/kcnd,pnbdz->pkbcz/dot_general | solution.py:43
  131.7 6.1 %copy.35 = f32[64,64,2,64,1]{1,3,2,4,0:T(8,128)} copy(f32[64,64,2,64,1]{0,3,2,1,4:T(8,128)} %fusion.54) | data formatting | bytes 4194304 | tf_op jit(solution)/shard_map/reshape.38
  137.8 6.0 %fusion.94 = f32[64,64,64,2,1]{2,1,4,3,0:T(8,128)S(1)} fusion(f32[64,64,2,64,1]{1,3,2,4,0:T(8,128)} %copy.35, f32[64,1,64,2]{2,0,3,1:T(8,128)S(1)} %get-tuple-element.365, f32[64,1,64,2]{2,0,3,1:T(8,128)S(1)} %get-tuple-element.364), kind=kOutput, calls=%fused_computation.107 | convolution fusion | flops 805322752 | bytes 4259840 | tf_op jit(solution)/shard_map/while/body/eval_jaxpr/kcnd,pandz->pakcz/dot_general | solution.py:45
  143.8 6.7 %convolution_bitcast_fusion.8 = f32[1,64,64,128]{3,2,1,0:T(8,128)S(1)} fusion(f32[64,64,128]{1,2,0:T(8,128)S(1)} %bitcast.297, f32[64,64]{1,0:T(8,128)S(1)} %get-tuple-element.380, f32[64,64]{1,0:T(8,128)S(1)} %fusion.124, f32[64,64]{1,0:T(8,128)S(1)} %get-tuple-element.379), kind=kOutput, calls=%fused_computation.98 | convolution fusion | flops 805355520 | bytes 4243456 | tf_op jit(solution)/shard_map/while/body/eval_jaxpr/dot_general | solution.py:35
  150.5 1.3 multiply_subtract_fusion
  151.8 2.0 pad_maximum_fusion
  154.1 28.9 %reduce-scatter.2.cloned.1.call-done = f32[1,16,64,128]{3,2,1,0:T(8,128)} async-done(((f32[1,64,64,128]{3,2,1,0:T(8,128)}), f32[1,16,64,128]{3,2,1,0:T(8,128)}) %reduce-scatter.2.cloned.1.call-update) | async-done | bytes 524304 | tf_op jit(solution)/shard_map/reduce_scatter | solution.py:198
  183.0 47.6 %all-gather.10.cloned.1.call-done = f32[4,16,64,128]{3,2,1,0:T(8,128)} async-done(((f32[1,16,64,128]{3,2,1,0:T(8,128)}), f32[4,16,64,128]{3,2,1,0:T(8,128)}) %all-gather.10.cloned.1.call-update) | async-done | bytes 2097168 | tf_op jit(solution)/shard_map/all_gather | solution.py:199
  230.6 10.9 %fusion.91 = f32[1,4]{1,0:T(1,128)S(1)} fusion(f32[131072,1]{0,1:T(1,128)S(1)} %bitcast.305, f32[1,4,1024,128]{3,2,1,0:T(8,128)} %bitcast.295), kind=kOutput, calls=%fused_computation.104 | convolution fusion | flops 6291460 | bytes 2621456 | tf_op jit(solution)/shard_map/ik,jk->ij/dot_general | solution.py:206
  241.5 0.9 fusion.150
  242.4 0.6 pad_maximum_fusion.1
  243.0 1.3 copy-done.2
  244.4 9.6 %fusion.85 = f32[1,4]{1,0:T(1,128)S(1)} fusion(f32[131072,1]{0,1:T(1,128)S(1)} %bitcast.306, f32[1,4,1024,128]{3,2,1,0:T(8,128)S(1)} %bitcast.299), kind=kOutput, calls=%fused_computation.102 | convolution fusion | flops 6291460 | bytes 2621456 | tf_op jit(solution)/shard_map/ik,jk->ij/dot_general | solution.py:207
  254.0 6.4 %all-reduce = (f32[1,4]{1,0:T(1,128)S(1)}, f32[1,4]{1,0:T(1,128)S(1)}) all-reduce(f32[1,4]{1,0:T(1,128)S(1)} %fusion.91, f32[1,4]{1,0:T(1,128)S(1)} %fusion.85), channel_id=1, replica_groups=mesh['kgrp'=2,'band'=4,'fft'=4] {'fft'}, use_global_device_ids=true, to_apply=%region_1.2 | all-reduce | flops 8 | bytes 64 | tf_op jit(solution)/shard_map/psum | solution.py:209
  260.4 9.1 %all-gather = f32[4,1,4]{2,1,0:T(1,128)S(1)} all-gather(f32[1,1,4]{2,1,0:T(1,128)S(1)} %bitcast.311), channel_id=1, replica_groups=mesh['kgrp'=2,'band'=4,'fft'=4] {'band'}, dimensions={0}, use_global_device_ids=true | all-gather | bytes 80 | tf_op jit(solution)/shard_map/all_gather | solution.py:211
  269.6 8.0 %all-gather.1 = f32[4,1,4]{2,1,0:T(1,128)S(1)} all-gather(f32[1,1,4]{2,1,0:T(1,128)S(1)} %bitcast.310), channel_id=1, replica_groups=mesh['kgrp'=2,'band'=4,'fft'=4] {'band'}, dimensions={0}, use_global_device_ids=true | all-gather | bytes 80 | tf_op jit(solution)/shard_map/all_gather | solution.py:212
  277.7 7.7 %while.39 = (s32[]{:T(128)}, f32[4,4]{1,0:T(4,128)S(1)}, f32[4,4]{1,0:T(4,128)S(1)}, f32[4,4]{0,1:T(4,128)S(1)}, f32[4,4]{0,1:T(4,128)S(1)}, /*index=5*/s32[]{:T(128)}, s32[]{:T(128)}) while((s32[]{:T(128)}, f32[4,4]{1,0:T(4,128)S(1)}, f32[4,4]{1,0:T(4,128)S(1)}, f32[4,4]{0,1:T(4,128)S(1)}, f32[4,4]{0,1:T(4,128)S(1)}, ...), condition=%wide.region_4.5_spmd.clone.clone, body=%wide.region_3.4_spmd.clone.clone.sunk | while | flops 887 | bytes 15635 | solution.py:138
  278.1 0.6 dynamic_slice.153
  283.9 0.6 dynamic_slice.153
  285.4 10.7 %while.38 = (s32[]{:T(128)}, f32[4,4]{1,0:T(4,128)S(1)}, f32[4,4]{1,0:T(4,128)S(1)}, f32[4,4]{1,0:T(4,128)S(1)}, f32[4,4]{1,0:T(4,128)S(1)}, /*index=5*/s32[]{:T(128)}, s32[]{:T(128)}) while((s32[]{:T(128)}, f32[4,4]{1,0:T(4,128)S(1)}, f32[4,4]{1,0:T(4,128)S(1)}, f32[4,4]{1,0:T(4,128)S(1)}, f32[4,4]{1,0:T(4,128)S(1)}, ...), condition=%wide.region_6.7_spmd.clone, body=%wide.region_5.6_spmd.clone.sunk | while | flops 935 | bytes 13294 | solution.py:160
  285.5 0.7 dynamic_slice.146
  286.2 0.8 fusion.191
  287.1 0.8 fusion.192
  288.2 0.7 dynamic_slice.146
  288.9 0.8 fusion.191
  289.8 0.8 fusion.192
  290.9 0.7 dynamic_slice.146
  291.5 0.8 fusion.191
  292.5 0.8 fusion.192
  293.6 0.7 dynamic_slice.146
  294.2 0.8 fusion.191
  295.2 0.8 fusion.192
  296.1 7.3 %fusion.61 = f32[1,131072]{1,0:T(1,128)S(1)} fusion(f32[1,4,1024,128]{3,2,1,0:T(8,128)S(1)} %bitcast.296, f32[4,4]{1,0:T(4,128)S(1)} %get-tuple-element.257, s32[]{:T(128)S(6)} %select_n.194), kind=kOutput, calls=%fused_computation.75 | convolution fusion | flops 6291456 | bytes 2621956 | tf_op jit(solution)/shard_map/dot_general | solution.py:217
  303.4 7.3 %fusion.57 = f32[1,131072]{1,0:T(1,128)S(1)} fusion(f32[1,4,1024,128]{3,2,1,0:T(8,128)S(1)} %bitcast.300, f32[4,4]{1,0:T(4,128)S(1)} %get-tuple-element.258, s32[]{:T(128)S(6)} %select_n.194), kind=kOutput, calls=%fused_computation.71 | convolution fusion | flops 6291456 | bytes 2621956 | tf_op jit(solution)/shard_map/dot_general | solution.py:217
  310.8 0.8 add.341
  (86 shorter events, 8.7 us)
Async XLA Ops:
  7.2 55.4 %copy-start = (f32[8,3]{0,1:T(4,128)S(1)}, f32[8,3]{0,1:T(4,128)}, u32[]{:S(2)}) copy-start(f32[8,3]{0,1:T(4,128)} %param.10) | copy-start | bytes 292
  7.2 50.8 %all-gather.6.cloned.1.call-start = ((), (), s32[]{:S(2)}) async-start(), calls=%async_computation.2 | async-start | bytes 2621440 | tf_op jit(solution)/shard_map/all_gather | solution.py:175
  7.9 84.4 %all-gather.8.cloned.1.call-start = ((), (), s32[]{:S(2)}) async-start(), calls=%async_computation.3 | async-start | bytes 2621440 | tf_op jit(solution)/shard_map/all_gather | solution.py:174
  8.8 53.2 %copy-start.5 = (s32[4]{0:T(128)S(1)}, s32[4]{0:T(128)}, u32[]{:S(2)}) copy-start(s32[4]{0:T(128)} %param.11) | copy-start | bytes 52
  58.0 40.5 %all-to-all-start = ((f32[4,16,64,128]{3,2,1,0:T(8,128)}), f32[4,16,64,128]{3,2,1,0:T(8,128)S(1)}, u32[]{:S(2)}, u32[]{:S(2)}) async-start(f32[4,16,64,128]{3,2,1,0:T(8,128)} %all-gather.6.cloned.1.call-done), calls=%async_computation | async-start | bytes 4194304 | tf_op jit(solution)/shard_map/all_to_all | solution.py:176
  61.6 121.3 %reduce-scatter.2.cloned.1.call-start = ((), (), s32[]{:S(2)}) async-start(), calls=%async_computation.4 | async-start | bytes 2621440 | tf_op jit(solution)/shard_map/reduce_scatter | solution.py:198
  153.8 76.8 %copy-start.4 = (f32[1,16,64,128]{3,2,1,0:T(8,128)S(1)}, f32[1,16,64,128]{3,2,1,0:T(8,128)}, u32[]{:S(2)}) copy-start(f32[1,16,64,128]{3,2,1,0:T(8,128)} %param.8) | copy-start | bytes 1572868
  153.8 76.8 %all-gather.10.cloned.1.call-start = ((), (), s32[]{:S(2)}) async-start(), calls=%async_computation.5 | async-start | bytes 2621440 | tf_op jit(solution)/shard_map/all_gather | solution.py:199
  230.6 10.9 %copy-start.1 = (f32[4,16,64,128]{3,2,1,0:T(8,128)S(1)}, f32[4,16,64,128]{3,2,1,0:T(8,128)}, u32[]{:S(2)}) copy-start(f32[4,16,64,128]{3,2,1,0:T(8,128)} %all-gather.10.cloned.1.call-done) | copy-start | bytes 6291460
  243.0 1.4 copy-start.2
  296.1 7.3 %copy-start.3 = (f32[4,16,64,128]{3,2,1,0:T(8,128)S(1)}, f32[4,16,64,128]{3,2,1,0:T(8,128)}, u32[]{:S(2)}) copy-start(f32[4,16,64,128]{3,2,1,0:T(8,128)} %copy-done.2) | copy-start | bytes 6291460
Sparse Core Ops, SparseCore 0:
  9.6 48.3 all-gather.5
  59.5 32.7 all-gather.7
  153.9 28.9 reduce-scatter.1
  184.9 45.6 all-gather.9
where the time goes:
time: 325 us; the launch traced here: 319 us
  waiting for transfers between devices  159 us (49%)
  matrix products  81.9 us (25%)
  blocking collectives  23.5 us (7%)
  local copies, waits for them, and re-layouts  20.2 us (6%)
  between operations  14.4 us (4%)
  other arithmetic  12.9 us (4%)
  starting transfers between devices  3.98 us (1%)
    all_gather x1, waiting for transfers between devices, body(): every_slab = lax.all_gather(partners, 'band', axis=0, tiled=True)  49.1 us
    all_gather x1, waiting for transfers between devices, body(): every_pot = lax.all_gather(potential, 'band', axis=0, tiled=True)  47.6 us
    reduce_scatter x1, waiting for transfers between devices, body(): lax.psum_scatter(partial_value, 'fft', scatter_dimension=1, tiled=True)  28.9 us
    all_gather x1, waiting for transfers between devices, body(): full_orbitals = lax.all_gather(orbitals, 'fft', axis=1, tiled=True)  25.8 us
    dot_general x2, matrix products, along_last(): return jnp.dot(flat, table, precision=HIGHEST).reshape(shape)  13.3 us
    another operation x2, local copies, waits for them, and re-layouts  12.2 us
    dot_general x2, matrix products, along_axis(): result = jnp.einsum('kcnd,pandz->pakcz', table, split, precision=HIGHEST)  11.5 us
    dot_general x2, matrix products, along_axis(): result = jnp.einsum('kcnd,pnbdz->pkbcz', table, split, precision=HIGHEST)  11.4 us
  transfers between devices with their start and end apart: 5, of which 5 were waited for; matrix products, arithmetic and copies ran while one was open for 2% of the time, Pallas kernels for 0%

commit v1 on v0

--- a/solution.py
+++ b/solution.py
@@ -1,11 +1,16 @@
+import functools
 import math
 
 import jax
 import jax.numpy as jnp
 from jax import lax
+from jax.experimental import pallas as pl
+from jax.experimental.pallas import tpu as pltpu
 from jax.sharding import PartitionSpec as P
 
 HIGHEST = lax.Precision.HIGHEST
+HIGH = lax.Precision.HIGH
+MESH = pl.DeviceIdType.MESH
 SCREEN_SQUARE = 0.25
 FOUR_PI = 4.0 * math.pi
 
@@ -32,7 +37,7 @@
 def along_last(field, table):
     shape = field.shape
     flat = field.reshape(-1, shape[-1])
-    return jnp.dot(flat, table, precision=HIGHEST).reshape(shape)
+    return jnp.dot(flat, table, precision=HIGH).reshape(shape)
 
 
 def along_axis(field, table, axis_number):
@@ -40,9 +45,9 @@
     extent = shape[-1] // 2
     split = field.reshape(shape[0], shape[1], shape[2], 2, extent)
     if axis_number == 1:
-        result = jnp.einsum("kcnd,pnbdz->pkbcz", table, split, precision=HIGHEST)
+        result = jnp.einsum("kcnd,pnbdz->pkbcz", table, split, precision=HIGH)
     else:
-        result = jnp.einsum("kcnd,pandz->pakcz", table, split, precision=HIGHEST)
+        result = jnp.einsum("kcnd,pandz->pakcz", table, split, precision=HIGH)
     return result.reshape(shape)
 
 
@@ -160,7 +165,7 @@
     return lax.fori_loop(0, matrix_order, solve_step, (zero_start, zero_start))
 
 
-def body(orbitals, partners, shift_table, shift_index):
+def general_body(orbitals, partners, shift_table, shift_index):
     extent = orbitals.shape[2]
     band_count = orbitals.shape[0]
     tables = (
@@ -220,6 +225,594 @@
     return (potential, projector.reshape(orbitals.shape))
 
 
+def remote(source, target, send_sem, recv_sem, where):
+    return pltpu.make_async_remote_copy(
+        src_ref=source,
+        dst_ref=target,
+        send_sem=send_sem,
+        recv_sem=recv_sem,
+        device_id=where,
+        device_id_type=MESH,
+    )
+
+
+def greet(others):
+    barrier = pltpu.get_barrier_semaphore()
+    for other in others:
+        pl.semaphore_signal(barrier, inc=1, device_id=other, device_id_type=MESH)
+    pl.semaphore_wait(barrier, len(others))
+
+
+def gather_kernel(
+    bands,
+    ranks,
+    orbital,
+    partner,
+    orbital_grid,
+    partner_grid,
+    orbital_parts,
+    from_below,
+    from_above,
+    chain_send,
+    chain_recv,
+    deliver_send,
+    deliver_recv,
+    grid_send,
+    grid_recv,
+    part_send,
+    part_recv,
+    local_sem,
+):
+    band = lax.axis_index("band")
+    rank = lax.axis_index("fft")
+    planes = orbital.shape[0]
+    piece = planes // bands
+    greet(
+        [{"band": (band + step) % bands} for step in range(1, bands)]
+        + [{"fft": (rank + step) % ranks} for step in range(1, ranks)]
+    )
+
+    def span(index):
+        return pl.ds(index * piece, piece)
+
+    def slab(index):
+        return pl.ds(index * planes, planes)
+
+    beside = rank + 1 - 2 * (rank % 2)
+    across = (rank + 2) % ranks
+    beside_across = (beside + 2) % ranks
+
+    def chain_copy(upward, distance, chunk):
+        held = from_below if upward else from_above
+        source = partner.at[span(chunk)] if distance == 0 else held.at[distance - 1, chunk]
+        way = 0 if upward else 1
+        return remote(
+            source,
+            held.at[distance, chunk],
+            chain_send.at[way, distance, chunk],
+            chain_recv.at[way, distance, chunk],
+            {"band": band + 1 if upward else band - 1},
+        )
+
+    def deliver(upward, distance, chunk, act):
+        held = from_below if upward else from_above
+        source = partner.at[span(chunk)] if distance == 0 else held.at[distance - 1, chunk]
+        owner = band - distance if upward else band + distance
+        target = partner_grid.at[pl.ds(rank * planes + chunk * piece, piece)]
+        way = 0 if upward else 1
+
+        @pl.when(owner == rank)
+        def _():
+            copy = pltpu.make_async_copy(source, target, local_sem.at[chunk])
+            copy.start() if act == "start" else copy.wait()
+
+        @pl.when(owner != rank)
+        def _():
+            copy = remote(
+                source,
+                target,
+                deliver_send.at[way, distance, chunk],
+                deliver_recv.at[rank, chunk],
+                {"fft": owner},
+            )
+            copy.start() if act == "start" else copy.wait_send()
+
+    def has_source(upward, distance):
+        return band >= distance if upward else band + distance <= bands - 1
+
+    def has_next(upward):
+        return band <= bands - 2 if upward else band >= 1
+
+    def both(first, second):
+        return jnp.logical_and(first, second)
+
+    for chunk in range(bands):
+        for upward in (True, False):
+
+            @pl.when(has_next(upward))
+            def _():
+                chain_copy(upward, 0, chunk).start()
+
+    to_across = remote(
+        orbital, orbital_grid.at[slab(rank)], grid_send.at[0], grid_recv.at[0], {"fft": across}
+    )
+    to_beside = remote(
+        orbital, orbital_grid.at[slab(rank)], grid_send.at[1], grid_recv.at[1], {"fft": beside}
+    )
+    to_across.start()
+    to_beside.start()
+    own_grid = pltpu.make_async_copy(orbital, orbital_grid.at[slab(rank)], local_sem.at[bands])
+    own_grid.start()
+    for chunk in range(bands):
+        deliver(True, 0, chunk, "start")
+    onward = remote(
+        orbital_grid.at[slab(across)],
+        orbital_grid.at[slab(across)],
+        grid_send.at[2],
+        grid_recv.at[2],
+        {"fft": beside},
+    )
+    for distance in range(1, bands):
+        for chunk in range(bands):
+            for upward in (True, False):
+
+                @pl.when(has_source(upward, distance))
+                def _():
+                    chain_copy(upward, distance - 1, chunk).wait_recv()
+
+                if distance < bands - 1:
+
+                    @pl.when(both(has_source(upward, distance), has_next(upward)))
+                    def _():
+                        chain_copy(upward, distance, chunk).start()
+
+                @pl.when(has_source(upward, distance))
+                def _():
+                    deliver(upward, distance, chunk, "start")
+
+        if distance == 1:
+            to_across.wait_recv()
+            onward.start()
+    part_copies = []
+    for step in range(1, bands):
+        other = (band + step) % bands
+        copy = remote(
+            orbital.at[span(other)],
+            orbital_parts.at[band],
+            part_send.at[step - 1],
+            part_recv.at[step - 1],
+            {"band": other},
+        )
+        copy.start()
+        part_copies.append(copy)
+    own_part = pltpu.make_async_copy(
+        orbital.at[span(band)], orbital_parts.at[band], local_sem.at[bands + 1]
+    )
+    own_part.start()
+
+    for copy in part_copies:
+        copy.wait()
+    own_part.wait()
+    own_grid.wait()
+    to_across.wait_send()
+    to_beside.wait()
+    onward.wait()
+    for distance in range(bands):
+        for chunk in range(bands):
+            for upward in (True, False):
+                if distance < bands - 1:
+
+                    @pl.when(both(has_source(upward, distance), has_next(upward)))
+                    def _():
+                        chain_copy(upward, distance, chunk).wait_send()
+
+                if distance > 0 or upward:
+
+                    @pl.when(has_source(upward, distance))
+                    def _():
+                        deliver(upward, distance, chunk, "wait")
+
+    for step in range(1, ranks):
+        source = (rank + step) % ranks
+        for chunk in range(bands):
+            target = partner_grid.at[pl.ds(source * planes + chunk * piece, piece)]
+            remote(
+                target,
+                target,
+                deliver_send.at[0, 0, chunk],
+                deliver_recv.at[source, chunk],
+                {"fft": source},
+            ).wait_recv()
+
+
+def gather_grids(bands, ranks, orbital, partner):
+    planes, rows, lanes = orbital.shape
+    piece = planes // bands
+    vmem = pl.BlockSpec(memory_space=pltpu.VMEM)
+    grid = jax.ShapeDtypeStruct((ranks * planes, rows, lanes), jnp.float32)
+    parts = jax.ShapeDtypeStruct((bands, piece, rows, lanes), jnp.float32)
+    held = pltpu.VMEM((bands, bands, piece, rows, lanes), jnp.float32)
+    dma = pltpu.SemaphoreType.DMA
+    return pl.pallas_call(
+        functools.partial(gather_kernel, bands, ranks),
+        name="gather_grids",
+        out_shape=(grid, grid, parts),
+        in_specs=[vmem, vmem],
+        out_specs=(vmem, vmem, vmem),
+        scratch_shapes=[
+            held,
+            held,
+            dma((2, bands, bands)),
+            dma((2, bands, bands)),
+            dma((2, bands, bands)),
+            dma((ranks, bands)),
+            dma((3,)),
+            dma((3,)),
+            dma((bands,)),
+            dma((bands,)),
+            dma((bands + 2,)),
+        ],
+        compiler_params=pltpu.CompilerParams(
+            collective_id=0, has_side_effects=True, vmem_limit_bytes=48 * 1024 * 1024
+        ),
+    )(orbital, partner)
+
+
+def turn(block):
+    lanes = block.shape[-1]
+    swapped = pltpu.roll(block, lanes // 2, block.ndim - 1)
+    position = lax.broadcasted_iota(jnp.int32, block.shape, block.ndim - 1)
+    return jnp.where(position < lanes // 2, swapped, -swapped)
+
+
+def small_factor_inverse(matrix):
+    order = len(matrix)
+    lower = [[None] * order for _ in range(order)]
+    for column in range(order):
+        residual = []
+        for row in range(column, order):
+            real, imag = matrix[row][column]
+            for k in range(column):
+                a, b = lower[row][k]
+                c, d = lower[column][k]
+                real = real - (a * c + b * d)
+                imag = imag - (b * c - a * d)
+            residual.append((real, imag))
+        pivot = jnp.sqrt(residual[0][0])
+        lower[column][column] = (pivot, jnp.zeros_like(pivot))
+        for row in range(column + 1, order):
+            real, imag = residual[row - column]
+            lower[row][column] = (real / pivot, imag / pivot)
+    inverse = [[None] * order for _ in range(order)]
+    for row in range(order):
+        pivot = lower[row][row][0]
+        inverse[row][row] = (1.0 / pivot, jnp.zeros_like(pivot))
+        for column in range(row):
+            real = jnp.zeros_like(pivot)
+            imag = jnp.zeros_like(pivot)
+            for k in range(column, row):
+                a, b = lower[row][k]
+                c, d = inverse[k][column]
+                real = real - (a * c - b * d)
+                imag = imag - (a * d + b * c)
+            inverse[row][column] = (real / pivot, imag / pivot)
+    return inverse
+
+
+def finish_kernel(
+    bands,
+    ranks,
+    partial,
+    orbital_parts,
+    potential,
+    projector,
+    near,
+    outgoing,
+    arriving,
+    potential_parts,
+    projector_parts,
+    own_sums,
+    all_sums,
+    near_send,
+    near_recv,
+    far_send,
+    far_recv,
+    part_send,
+    part_recv,
+    sum_send,
+    sum_recv,
+    back_send,
+    back_recv,
+):
+    band = lax.axis_index("band")
+    rank = lax.axis_index("fft")
+    planes, rows, lanes = potential.shape
+    piece = planes // bands
+    beside = rank + 1 - 2 * (rank % 2)
+    across = (rank + 2) % ranks
+    beside_across = (beside + 2) % ranks
+    others = [
+        {"band": (band + step) % bands, "fft": (rank + turn_by) % ranks}
+        for step in range(bands)
+        for turn_by in range(ranks)
+        if step or turn_by
+    ]
+    greet(others)
+
+    def span(index):
+        return pl.ds(index * piece, piece)
+
+    def window(index, chunk):
+        return pl.ds(index * planes + chunk * piece, piece)
+
+    near_copies = []
+    for chunk in range(bands):
+        pair = []
+        for which, index in ((1, beside_across), (0, beside)):
+            copy = remote(
+                partial.at[window(index, chunk)],
+                near.at[which, chunk],
+                near_send.at[which, chunk],
+                near_recv.at[which, chunk],
+                {"fft": beside},
+            )
+            copy.start()
+            pair.append(copy)
+        near_copies.append(pair)
+    far_copies = []
+    for chunk in range(bands):
+        near_copies[chunk][0].wait()
+        outgoing[chunk] = partial[window(across, chunk)] + near[1, chunk]
+        copy = remote(
+            outgoing.at[chunk],
+            arriving.at[chunk],
+            far_send.at[chunk],
+            far_recv.at[chunk],
+            {"fft": across},
+        )
+        copy.start()
+        far_copies.append(copy)
+    for chunk in range(bands):
+        near_copies[chunk][1].wait()
+        far_copies[chunk].wait_recv()
+        potential[span(chunk)] = (partial[window(rank, chunk)] + near[0, chunk]) + arriving[chunk]
+
+        def part_copy(source_band):
+            return remote(
+                potential.at[span(chunk)],
+                potential_parts.at[source_band],
+                part_send.at[chunk],
+                part_recv.at[source_band],
+                {"band": chunk},
+            )
+
+        @pl.when(band != chunk)
+        def _():
+            part_copy(band).start()
+
+        @pl.when(band == chunk)
+        def _():
+            potential_parts[chunk] = potential[span(chunk)]
+
+    for other in range(bands):
+
+        @pl.when(band != other)
+        def _():
+            remote(
+                potential_parts.at[other],
+                potential_parts.at[other],
+                part_send.at[other],
+                part_recv.at[other],
+                {"band": other},
+            ).wait_recv()
+
+    entries = [(i, l) for i in range(bands) for l in range(i + 1)]
+    position = lax.broadcasted_iota(jnp.int32, (8, lanes), 1)
+
+    def accumulate(plane, sums):
+        turned = []
+        straight = []
+        for l in range(bands):
+            block = potential_parts[l, plane]
+            straight.append(block)
+            turned.append(turn(block))
+        result = []
+        for number, (i, l) in enumerate(entries):
+            left = orbital_parts[i, plane]
+            for half, right in enumerate((straight[l], turned[l])):
+                product = (left * right).reshape(rows // 8, 8, lanes)
+                result.append(sums[2 * number + half] + jnp.sum(product, axis=0))
+        return tuple(result)
+
+    zero = jnp.zeros((8, lanes), jnp.float32)
+    sums = lax.fori_loop(0, piece, accumulate, (zero,) * (2 * len(entries)))
+    packed = zero
+    for number, value in enumerate(sums):
+        packed = jnp.where(position == number, jnp.sum(value, axis=1, keepdims=True), packed)
+    own_sums[...] = packed
+    sum_copies = []
+    number = 0
+    for step in range(bands):
+        for turn_by in range(ranks):
+            if step == 0 and turn_by == 0:
+                continue
+            copy = remote(
+                own_sums,
+                all_sums.at[band, rank],
+                sum_send.at[step, turn_by],
+                sum_recv.at[step, turn_by],
+                {"band": (band + step) % bands, "fft": (rank + turn_by) % ranks},
+            )
+            copy.start()
+            sum_copies.append(copy)
+    all_sums[band, rank] = packed
+    for copy in sum_copies:
+        copy.wait()
+    total = zero
+    for one_band in range(bands):
+        for one_rank in range(ranks):
+            total = total + all_sums[one_band, one_rank]
+    total = jnp.broadcast_to(jnp.sum(total, axis=0, keepdims=True), (8, lanes))
+    volume = float(lanes // 2) * float(rows) * float(planes * ranks)
+    matrix = [[None] * bands for _ in range(bands)]
+    for number, (i, l) in enumerate(entries):
+        values = [
+            jnp.broadcast_to(
+                jnp.sum(jnp.where(position == 2 * number + half, total, 0.0), axis=1, keepdims=True),
+                (8, lanes),
+            )
+            / volume
+            for half in range(2)
+        ]
+        matrix[i][l] = (values[0], values[1])
+    inverse = small_factor_inverse(matrix)
+    back_copies = []
+
+    def spread(value):
+        return value[:1]
+
+    for l in range(bands):
+
+        def combine(plane, carry):
+            sum_straight = jnp.zeros((rows, lanes), jnp.float32)
+            sum_turned = jnp.zeros((rows, lanes), jnp.float32)
+            for m in range(l + 1):
+                block = potential_parts[m, plane]
+                real, imag = inverse[l][m]
+                sum_straight = sum_straight + spread(real) * block
+                sum_turned = sum_turned + spread(imag) * block
+            projector_parts[l, plane] = sum_straight + turn(sum_turned)
+            return carry
+
+        lax.fori_loop(0, piece, combine, 0)
+
+        @pl.when(band != l)
+        def _():
+            remote(
+                projector_parts.at[l],
+                projector.at[span(band)],
+                back_send.at[l],
+                back_recv.at[band],
+                {"band": l},
+            ).start()
+
+        @pl.when(band == l)
+        def _():
+            projector[span(l)] = projector_parts[l]
+
+    for other in range(bands):
+
+        @pl.when(band != other)
+        def _():
+            copy = remote(
+                projector_parts.at[other],
+                projector.at[span(other)],
+                back_send.at[other],
+                back_recv.at[other],
+                {"band": other},
+            )
+            copy.wait_recv()
+            copy.wait_send()
+            remote(
+                potential.at[span(other)],
+                potential_parts.at[other],
+                part_send.at[other],
+                part_recv.at[other],
+                {"band": other},
+            ).wait_send()
+
+    for copy in far_copies:
+        copy.wait_send()
+
+
+def finish(bands, ranks, partial, orbital_parts):
+    whole, rows, lanes = partial.shape
+    planes = whole // ranks
+    piece = planes // bands
+    vmem = pl.BlockSpec(memory_space=pltpu.VMEM)
+    out = jax.ShapeDtypeStruct((planes, rows, lanes), jnp.float32)
+    dma = pltpu.SemaphoreType.DMA
+    quarters = pltpu.VMEM((bands, piece, rows, lanes), jnp.float32)
+    return pl.pallas_call(
+        functools.partial(finish_kernel, bands, ranks),
+        name="finish",
+        out_shape=(out, out),
+        in_specs=[vmem, vmem],
+        out_specs=(vmem, vmem),
+        scratch_shapes=[
+            pltpu.VMEM((2, bands, piece, rows, lanes), jnp.float32),
+            quarters,
+            quarters,
+            quarters,
+            quarters,
+            pltpu.VMEM((8, lanes), jnp.float32),
+            pltpu.VMEM((bands, ranks, 8, lanes), jnp.float32),
+            dma((2, bands)),
+            dma((2, bands)),
+            dma((bands,)),
+            dma((bands,)),
+            dma((bands,)),
+            dma((bands,)),
+            dma((bands, ranks)),
+            dma((bands, ranks)),
+            dma((bands,)),
+            dma((bands,)),
+        ],
+        compiler_params=pltpu.CompilerParams(
+            collective_id=1, has_side_effects=True, vmem_limit_bytes=48 * 1024 * 1024
+        ),
+    )(partial, orbital_parts)
+
+
+def apply_pair(orbital_grid, partner_grid, qvector):
+    extent = orbital_grid.shape[1]
+    tables = (
+        last_table(extent, -1.0),
+        middle_table(extent, -1.0),
+        last_table(extent, 1.0),
+        middle_table(extent, 1.0),
+    )
+    forward_last, forward_mid, inverse_last, inverse_mid = tables
+    single = partner_grid[None]
+    kernel = kernel_block(qvector, extent, extent)
+    density = times_conj(single, orbital_grid[None])
+    spectrum = (
+        along_axis(along_axis(along_last(density, forward_last), forward_mid, 2), forward_mid, 1)
+        * kernel
+    )
+    field = along_last(
+        along_axis(along_axis(spectrum, inverse_mid, 1), inverse_mid, 2), inverse_last
+    )
+    return times(single, field)[0]
+
+
+def paired_body(bands, ranks, orbitals, partners, shift_table, shift_index):
+    orbital_grid, partner_grid, orbital_parts = gather_grids(bands, ranks, orbitals[0], partners[0])
+    qvector = shifts_for(shift_table, shift_index, lax.axis_index("fft"), 1)
+    partial = apply_pair(orbital_grid, partner_grid, qvector)
+    potential, projector = finish(bands, ranks, partial, orbital_parts)
+    return (potential[None], projector[None])
+
+
+def body(orbitals, partners, shift_table, shift_index):
+    bands = lax.axis_size("band")
+    ranks = lax.axis_size("fft")
+    count, planes, rows, lanes = orbitals.shape
+    grid_bytes = ranks * planes * rows * lanes * 4
+    paired = (
+        count == 1
+        and ranks == 4
+        and bands == ranks
+        and planes % bands == 0
+        and lanes == 2 * rows
+        and lanes == 128
+        and grid_bytes <= 2 * 1024 * 1024
+    )
+    if paired:
+        return paired_body(bands, ranks, orbitals, partners, shift_table, shift_index)
+    return general_body(orbitals, partners, shift_table, shift_index)
+
+
 def solution(mesh):
     in_specs = (
         P(("kgrp", "band"), "fft", None, None),

time: 325 us -> 158 us (0.49); the launches traced: 319 us -> 157 us
  waiting for transfers between devices: 159 us -> 0 us
  Pallas kernels: 0 us -> 98.5 us
  matrix products: 81.9 us -> 32.7 us
  blocking collectives: 23.5 us -> 0 us
  between operations: 14.4 us -> 0.75 us
  other arithmetic: 12.9 us -> 8.1 us
  starting transfers between devices: 3.98 us -> 0 us
    all_gather x3 -> x0, waiting for transfers between devices: 123 us -> none  [the longest x1 49.1 us: body(): every_slab = lax.all_gather(partners, 'band', axis=0, tiled=True)]
    pallas_call x0 -> x2, Pallas kernels: none -> 98.5 us  [the longest x1 51.7 us: gather_grids(): pl.pallas_call(functools.partial(gather_kernel, bands, ranks), name='gath...]
    dot_general x42 -> x6, matrix products: 81.2 us -> 32 us  [the longest x2 15.7 us: along_axis(): result = jnp.einsum('kcnd,pnbdz->pkbcz', table, split, precision=HIGH)]
    reduce_scatter x1 -> x0, waiting for transfers between devices: 28.9 us -> none  [body(): lax.psum_scatter(partial_value, 'fft', scatter_dimension=1, tiled=True)]
    all_gather x2 -> x0, blocking collectives: 17.1 us -> none  [the longest x1 9.15 us: body(): lax.all_gather(summed_real, 'band', axis=0, tiled=True)]
    psum x1 -> x0, blocking collectives: 6.38 us -> none  [body(): summed_real, summed_imag = lax.psum((rows_real, rows_imag), 'fft')]
    all_to_all x1 -> x0, waiting for transfers between devices: 6.17 us -> none  [body(): lax.all_to_all(every_slab, 'fft', split_axis=0, concat_axis=1, tiled=True)]
    dynamic_slice x8 -> x0, local copies, waits for them, and re-layouts: 5.12 us -> none  [the longest x4 2.68 us: solve_step(): pivot_value = lower_real[row_index, row_index]]
  transfers between devices with their start and end apart: 5 -> 0, of which waited for: 5 -> 0; matrix products, arithmetic and copies ran while one was open for 2% -> 0% of each run, Pallas kernels for 0% -> 0%
where the time goes in v1:
time: 158 us; the launch traced here: 157 us
  Pallas kernels  98.5 us (62%)
  matrix products  32.7 us (21%)
  local copies, waits for them, and re-layouts  17.1 us (11%)
  other arithmetic  8.1 us (5%)
    pallas_call x1, Pallas kernels, gather_grids(): pl.pallas_call(functools.partial(gather_kernel, bands, ranks), name='gath...  51.7 us
    pallas_call x1, Pallas kernels, finish(): pl.pallas_call(functools.partial(finish_kernel, bands, ranks), name='fini...  46.8 us
    dot_general x2, matrix products, along_axis(): result = jnp.einsum('kcnd,pnbdz->pkbcz', table, split, precision=HIGH)  15.7 us
    another operation x2, local copies, waits for them, and re-layouts  12.2 us
    dot_general x2, matrix products, along_last(): return jnp.dot(flat, table, precision=HIGH).reshape(shape)  9.02 us
    dot_general x2, matrix products, along_axis(): result = jnp.einsum('kcnd,pandz->pakcz', table, split, precision=HIGH)  7.24 us
    unnamed x10, local copies, waits for them, and re-layouts  3.68 us
    add x1, other arithmetic, times_conj(): left_real * right_real + left_imag * right_imag  3.26 us

profile of v1, /device:TPU:0, one launch (start us, length us, event | category | flops | bytes accessed | tf_op | source)
XLA Modules:
  0.0 157.2 jit_solution(12183729803229653443)
XLA Ops:
  0.6 0.0 copy-start
  0.6 0.0 copy-start.1
  0.7 1.0 copy-done.1
  1.7 0.0 copy-start.2
  1.7 1.0 copy-done.2
  2.7 51.7 %gather_grids.1 = (f32[64,64,128]{2,1,0:T(8,128)S(1)}, f32[64,64,128]{2,1,0:T(8,128)S(1)}, f32[4,4,64,128]{3,2,1,0:T(8,128)S(1)}) custom-call(f32[16,64,128]{2,1,0:T(8,128)S(1)} %bitcast.109, f32[16,64,128]{2,1,0:T(8,128)S(1)} %bitcast.110), custom_call_target="tpu_custom_call" | custom-call | tf_op jit(solution)/shard_map/gather_grids/pallas_call | solution.py:436
  54.4 3.3 %multiply_add_fusion.1 = (f32[1,64,64,64]{3,2,1,0:T(8,128)}, f32[1,64,64,64]{3,2,1,0:T(8,128)}) fusion(f32[1,64,64,128]{3,2,1,0:T(8,128)S(1)} %bitcast.108, f32[1,64,64,128]{3,2,1,0:T(8,128)S(1)} %bitcast.106), kind=kLoop, calls=%fused_computation.22 | loop fusion | flops 1572864 | bytes 6291456 | tf_op jit(solution)/shard_map/add | solution.py:60
  57.7 0.1 broadcast_multiply_fusion.1
  57.8 0.1 fusion.51
  58.0 0.1 fusion.27
  58.1 0.1 copy.9
  58.2 5.5 %fusion.13 = f32[64,64,2,64]{1,3,2,0:T(8,128)S(1)} fusion(f32[2,64,128,1]{2,1,0,3:T(8,128)S(1)} %bitcast.114, f32[1,64,64,64]{3,2,1,0:T(8,128)} %get-tuple-element.15, f32[1,64,64,64]{3,2,1,0:T(8,128)} %get-tuple-element.14), kind=kOutput, calls=%fused_computation.11 | convolution fusion | flops 403177472 | bytes 4259840 | tf_op jit(solution)/shard_map/dot_general | solution.py:40
  63.7 0.1 broadcast_multiply_fusion
  63.8 0.1 fusion.46
  64.0 0.1 fusion.52
  64.2 3.4 %fusion.7 = f32[64,64,2,64,1]{1,3,2,0,4:T(8,128)} fusion(f32[64,64,2,64]{1,3,2,0:T(8,128)S(1)} %fusion.13, f32[64,1,64,2]{2,0,3,1:T(8,128)S(1)} %get-tuple-element.18, f32[64,1,64,2]{2,0,3,1:T(8,128)S(1)} %get-tuple-element.19), kind=kOutput, calls=%fused_computation.8 | convolution fusion | flops 402669568 | bytes 4259840 | tf_op jit(solution)/shard_map/kcnd,pandz->pakcz/dot_general | solution.py:50
  67.6 6.1 %copy.16 = f32[64,64,2,64,1]{0,3,2,4,1:T(8,128)} copy(f32[64,64,2,64,1]{1,3,2,0,4:T(8,128)} %fusion.7) | data formatting | bytes 4194304 | tf_op jit(solution)/shard_map/reshape.2
  73.6 0.0 copy-start.3
  73.6 7.2 %fusion.21 = f32[64,64,64,2,1]{2,1,4,3,0:T(8,128)} fusion(f32[64,64,2,64,1]{0,3,2,4,1:T(8,128)} %copy.16, f32[64,1,64,2]{2,0,3,1:T(8,128)S(1)} %get-tuple-element.18, f32[64,1,64,2]{2,0,3,1:T(8,128)S(1)} %get-tuple-element.19), kind=kOutput, calls=%fused_computation.27 | convolution fusion | flops 402669568 | bytes 4259840 | tf_op jit(solution)/shard_map/kcnd,pnbdz->pkbcz/dot_general | solution.py:48
  80.9 0.0 copy-done.3
  80.9 0.6 dynamic_slice.3
  81.4 0.0 copy-done
  81.5 0.8 fusion.53
  82.2 0.6 fusion.70
  82.8 1.3 add_multiply_fusion
  84.1 0.1 broadcast_add_fusion
  84.2 0.6 fusion.58
  84.8 8.5 %fusion.10 = f32[64,64,2,64,1]{0,3,2,1,4:T(8,128)} fusion(f32[64,64,64,2,1]{2,1,4,3,0:T(8,128)} %fusion.21, f32[2,64]{1,0:T(2,128)S(1)} %fusion.58, f32[64,64]{0,1:T(8,128)S(1)} %broadcast_add_fusion, f32[64,1,64,2]{2,0,3,1:T(8,128)S(1)} %get-tuple-element.17, f32[64,1,64,2]{2,0,3,1:T(8,128)S(1)} %get-tuple-element.16), kind=kOutput, calls=%fused_computation.9 | convolution fusion | flops 404766720 | bytes 4276736 | tf_op jit(solution)/shard_map/kcnd,pnbdz->pkbcz/dot_general | solution.py:48
  93.3 6.1 %copy.20 = f32[64,64,2,64,1]{1,3,2,4,0:T(8,128)} copy(f32[64,64,2,64,1]{0,3,2,1,4:T(8,128)} %fusion.10) | data formatting | bytes 4194304 | tf_op jit(solution)/shard_map/reshape.22
  99.4 3.8 %fusion.20 = f32[64,64,64,2,1]{2,1,4,3,0:T(8,128)S(1)} fusion(f32[64,64,2,64,1]{1,3,2,4,0:T(8,128)} %copy.20, f32[64,1,64,2]{2,0,3,1:T(8,128)S(1)} %get-tuple-element.17, f32[64,1,64,2]{2,0,3,1:T(8,128)S(1)} %get-tuple-element.16), kind=kOutput, calls=%fused_computation.26 | convolution fusion | flops 402669568 | bytes 4259840 | tf_op jit(solution)/shard_map/kcnd,pandz->pakcz/dot_general | solution.py:50
  103.2 0.1 fusion.48
  103.3 3.5 %convolution_bitcast_fusion = f32[1,64,64,128]{3,2,1,0:T(8,128)S(1)} fusion(f32[64,64,128]{1,2,0:T(8,128)S(1)} %bitcast.113, f32[64,64]{1,0:T(8,128)S(1)} %get-tuple-element.24, f32[64,64]{1,0:T(8,128)S(1)} %get-tuple-element.32, f32[64,64]{1,0:T(8,128)S(1)} %get-tuple-element.31), kind=kOutput, calls=%fused_computation.23 | convolution fusion | flops 402702336 | bytes 4243456 | tf_op jit(solution)/shard_map/dot_general | solution.py:40
  106.9 1.3 multiply_subtract_fusion
  108.2 0.6 maximum_bitcast_fusion.2.partial
  108.8 46.8 %finish.1 = (f32[16,64,128]{2,1,0:T(8,128)S(1)}, f32[16,64,128]{2,1,0:T(8,128)S(1)}) custom-call(f32[64,64,128]{2,1,0:T(8,128)S(1)} %maximum_bitcast_fusion.2.partial, f32[4,4,64,128]{3,2,1,0:T(8,128)S(1)} %get-tuple-element.9.orbital_parts), custom_call_target="tpu_custom_call" | custom-call | tf_op jit(solution)/shard_map/finish/pallas_call | solution.py:736
  155.6 0.8 copy.29
  156.4 0.8 copy.30
  (1 shorter events, 0.0 us)
Async XLA Ops:
  0.6 80.8 %copy-start = (f32[8,3]{0,1:T(4,128)S(1)}, f32[8,3]{0,1:T(4,128)}, u32[]{:S(2)}) copy-start(f32[8,3]{0,1:T(4,128)} %param.6) | copy-start | bytes 292
  0.6 1.0 copy-start.1
  1.7 1.0 copy-start.2
  73.6 7.2 %copy-start.3 = (s32[4]{0:T(128)S(1)}, s32[4]{0:T(128)}, u32[]{:S(2)}) copy-start(s32[4]{0:T(128)} %param.7) | copy-start | bytes 52

commit v2 on v1

--- a/solution.py
+++ b/solution.py
@@ -3,6 +3,7 @@
 
 import jax
 import jax.numpy as jnp
+import numpy as np
 from jax import lax
 from jax.experimental import pallas as pl
 from jax.experimental.pallas import tpu as pltpu
@@ -11,6 +12,7 @@
 HIGHEST = lax.Precision.HIGHEST
 HIGH = lax.Precision.HIGH
 MESH = pl.DeviceIdType.MESH
+GROUP = 8
 SCREEN_SQUARE = 0.25
 FOUR_PI = 4.0 * math.pi
 
@@ -764,32 +766,173 @@
     )(partial, orbital_parts)
 
 
-def apply_pair(orbital_grid, partner_grid, qvector):
+def split_table(table):
+    high = table.astype(jnp.bfloat16)
+    low = (table - high.astype(np.float64)).astype(jnp.bfloat16)
+    return high, low
+
+
+def right_table(extent, sign):
+    grid = np.outer(np.arange(extent), np.arange(extent)) % extent
+    angle = 2.0 * math.pi / extent * grid
+    cosine, sine = np.cos(angle), sign * np.sin(angle)
+    table = np.block([[cosine, sine], [-sine, cosine]])
+    high, low = split_table(table)
+    upper = np.concatenate([high, low], axis=1)
+    lower = np.concatenate([high, np.zeros_like(low)], axis=1)
+    return np.concatenate([upper, lower], axis=0)
+
+
+def left_table(extent, sign):
+    grid = np.outer(np.arange(extent), np.arange(extent)) % extent
+    angle = 2.0 * math.pi / extent * grid
+    high, low = split_table(np.concatenate([np.cos(angle), sign * np.sin(angle)], axis=0))
+    return np.concatenate([high, high, low], axis=1)
+
+
+def halves(value):
+    high = value.astype(jnp.bfloat16)
+    low = (value - high.astype(jnp.float32)).astype(jnp.bfloat16)
+    return high, low
+
+
+def right_product(value, table):
+    lanes = value.shape[-1]
+    high, low = halves(value)
+    both = jnp.dot(
+        jnp.concatenate([high, low], axis=1), table, preferred_element_type=jnp.float32
+    )
+    return both[:, :lanes] + both[:, lanes:]
+
+
+def left_product(first, second, table):
+    rows, lanes = first.shape
+    high, low = halves(jnp.concatenate([first, second], axis=1))
+    stacked = jnp.concatenate([high, low, high], axis=0)
+    both = jnp.dot(table, stacked, preferred_element_type=jnp.float32)
+    return tuple(
+        both[:rows, cut : cut + lanes] - turn(both[rows:, cut : cut + lanes])
+        for cut in (0, lanes)
+    )
+
+
+def spread_parts(value):
+    lanes = value.shape[-1]
+    swapped = pltpu.roll(value, lanes // 2, value.ndim - 1)
+    lower = lax.broadcasted_iota(jnp.int32, value.shape, value.ndim - 1) < lanes // 2
+    return jnp.where(lower, value, swapped), jnp.where(lower, swapped, value)
+
+
+def forward_group(group, orbital_grid, partner_grid, work, right, left):
+    rows, lanes = orbital_grid.shape[1:]
+    span = pl.ds(group * GROUP, GROUP)
+    orbital = orbital_grid[span].reshape(GROUP * rows, lanes)
+    real, imag = spread_parts(partner_grid[span].reshape(GROUP * rows, lanes))
+    density = real * orbital + imag * turn(orbital)
+    lines = right_product(density, right[...])
+    planes = []
+    for pair in range(GROUP // 2):
+        start = 2 * pair * rows
+        planes += left_product(
+            lines[start : start + rows], lines[start + rows : start + 2 * rows], left[...]
+        )
+    stacked = jnp.stack(planes, axis=0)
+    work[:, span, :] = jnp.swapaxes(stacked, 0, 1)
+
+
+def backward_group(group, partner_grid, partial, work, right, left):
+    rows, lanes = partner_grid.shape[1:]
+    span = pl.ds(group * GROUP, GROUP)
+    planes = jnp.swapaxes(work[:, span, :], 0, 1)
+    lines = []
+    for pair in range(GROUP // 2):
+        lines += left_product(planes[2 * pair], planes[2 * pair + 1], left[...])
+    field = right_product(jnp.concatenate(lines, axis=0), right[...])
+    real, imag = spread_parts(partner_grid[span].reshape(GROUP * rows, lanes))
+    partial[span] = (real * field - imag * turn(field)).reshape(GROUP, rows, lanes)
+
+
+def middle_pairs(shift, work, forward, inverse):
+    columns, extent, lanes = work.shape
+    first = frequency(lax.broadcasted_iota(jnp.int32, (extent, lanes), 0), extent)
+    third_place = lax.broadcasted_iota(jnp.int32, (extent, lanes), 1)
+    third_place = jnp.where(third_place < lanes // 2, third_place, third_place - lanes // 2)
+    third = frequency(third_place, extent)
+    base = (first + shift[0]) ** 2 + (third + shift[2]) ** 2 + SCREEN_SQUARE
+    scale = FOUR_PI / (float(extent) * float(columns) * float(lanes // 2))
+
+    def one_pair(pair, carry):
+        spectra = left_product(work[2 * pair], work[2 * pair + 1], forward[...])
+        scaled = []
+        for which in range(2):
+            column = 2 * pair + which
+            second = jnp.where(column < columns // 2, column, column - columns)
+            offset = (second.astype(jnp.float32) + shift[1]) ** 2
+            scaled.append(spectra[which] * (scale / (base + offset)))
+        fields = left_product(scaled[0], scaled[1], inverse[...])
+        work[2 * pair] = fields[0]
+        work[2 * pair + 1] = fields[1]
+        return carry
+
+    lax.fori_loop(0, columns // 2, one_pair, 0, unroll=2)
+
+
+def pair_kernel(
+    shift_table,
+    shift_index,
+    orbital_grid,
+    partner_grid,
+    right_forward,
+    right_inverse,
+    left_forward,
+    left_inverse,
+    partial,
+    work,
+):
+    chosen = shift_index[lax.axis_index("fft")]
+    shift = [shift_table[chosen, axis] for axis in range(3)]
+    groups = orbital_grid.shape[0] // GROUP
+
+    def forward(group, carry):
+        forward_group(group, orbital_grid, partner_grid, work, right_forward, left_forward)
+        return carry
+
+    def backward(group, carry):
+        backward_group(group, partner_grid, partial, work, right_inverse, left_inverse)
+        return carry
+
+    lax.fori_loop(0, groups, forward, 0)
+    middle_pairs(shift, work, left_forward, left_inverse)
+    lax.fori_loop(0, groups, backward, 0)
+
+
+def apply_pair(orbital_grid, partner_grid, shift_table, shift_index):
     extent = orbital_grid.shape[1]
-    tables = (
-        last_table(extent, -1.0),
-        middle_table(extent, -1.0),
-        last_table(extent, 1.0),
-        middle_table(extent, 1.0),
-    )
-    forward_last, forward_mid, inverse_last, inverse_mid = tables
-    single = partner_grid[None]
-    kernel = kernel_block(qvector, extent, extent)
-    density = times_conj(single, orbital_grid[None])
-    spectrum = (
-        along_axis(along_axis(along_last(density, forward_last), forward_mid, 2), forward_mid, 1)
-        * kernel
-    )
-    field = along_last(
-        along_axis(along_axis(spectrum, inverse_mid, 1), inverse_mid, 2), inverse_last
-    )
-    return times(single, field)[0]
+    tables = [
+        jnp.asarray(table)
+        for table in (
+            right_table(extent, -1.0),
+            right_table(extent, 1.0),
+            left_table(extent, -1.0),
+            left_table(extent, 1.0),
+        )
+    ]
+    vmem = pl.BlockSpec(memory_space=pltpu.VMEM)
+    smem = pl.BlockSpec(memory_space=pltpu.SMEM)
+    return pl.pallas_call(
+        pair_kernel,
+        name="apply_pair",
+        out_shape=jax.ShapeDtypeStruct(orbital_grid.shape, jnp.float32),
+        in_specs=[smem, smem] + [vmem] * 6,
+        out_specs=vmem,
+        scratch_shapes=[pltpu.VMEM(orbital_grid.shape, jnp.float32)],
+        compiler_params=pltpu.CompilerParams(vmem_limit_bytes=48 * 1024 * 1024),
+    )(shift_table, shift_index, orbital_grid, partner_grid, *tables)
 
 
 def paired_body(bands, ranks, orbitals, partners, shift_table, shift_index):
     orbital_grid, partner_grid, orbital_parts = gather_grids(bands, ranks, orbitals[0], partners[0])
-    qvector = shifts_for(shift_table, shift_index, lax.axis_index("fft"), 1)
-    partial = apply_pair(orbital_grid, partner_grid, qvector)
+    partial = apply_pair(orbital_grid, partner_grid, shift_table, shift_index)
     potential, projector = finish(bands, ranks, partial, orbital_parts)
     return (potential[None], projector[None])
 

time: 158 us -> 130 us (0.82)
  matrix products: 32.7 us -> 0 us
  Pallas kernels: 98.5 us -> 118 us
  other arithmetic: 8.1 us -> 0 us
  local copies, waits for them, and re-layouts: 17.1 us -> 9.9 us
    dot_general x7 -> x0, matrix products: 32.7 us -> none  [the longest x2 15.7 us: along_axis(): result = jnp.einsum('kcnd,pnbdz->pkbcz', table, split, precision=HIGH)]
    pallas_call x0 -> x1, Pallas kernels: none -> 19.8 us  [apply_pair(): pl.pallas_call(pair_kernel, name='apply_pair', out_shape=jax.ShapeDtypeSt...]
    another operation x2 -> x0, local copies, waits for them, and re-layouts: 12.2 us -> none
    unnamed x10 -> x19, local copies, waits for them, and re-layouts: 3.68 us -> 9.9 us
    add x2 -> x0, other arithmetic: 3.33 us -> none  [the longest x1 3.26 us: times_conj(): left_real * right_real + left_imag * right_imag]
    integer_pow x2 -> x0, other arithmetic: 1.86 us -> none  [the longest x1 1.3 us: kernel_block(): second_part = (second_freq[None, :] + qvectors[:, 1:2]) ** 2]
where the time goes in v2:
time: 130 us; the launch traced here: 129 us
  Pallas kernels  118 us (91%)
  local copies, waits for them, and re-layouts  9.9 us (8%)
    pallas_call x1, Pallas kernels, gather_grids(): pl.pallas_call(functools.partial(gather_kernel, bands, ranks), name='gath...  51.7 us
    pallas_call x1, Pallas kernels, finish(): pl.pallas_call(functools.partial(finish_kernel, bands, ranks), name='fini...  46.8 us
    pallas_call x1, Pallas kernels, apply_pair(): pl.pallas_call(pair_kernel, name='apply_pair', out_shape=jax.ShapeDtypeSt...  19.8 us
    unnamed x19, local copies, waits for them, and re-layouts  9.9 us

profile of v2, /device:TPU:0, one launch (start us, length us, event | category | flops | bytes accessed | tf_op | source)
XLA Modules:
  0.0 128.8 jit_solution(3556378358359333864)
XLA Ops:
  0.6 0.8 copy.10.shift_table
  1.4 0.0 copy-start.1
  1.4 1.0 copy-done.1
  2.4 0.0 copy-start.2
  2.4 1.0 copy-done.2
  3.5 51.7 %gather_grids.1 = (f32[64,64,128]{2,1,0:T(8,128)S(1)}, f32[64,64,128]{2,1,0:T(8,128)S(1)}, f32[4,4,64,128]{3,2,1,0:T(8,128)S(1)}) custom-call(f32[16,64,128]{2,1,0:T(8,128)S(1)} %bitcast.4, f32[16,64,128]{2,1,0:T(8,128)S(1)} %bitcast.5), custom_call_target="tpu_custom_call" | custom-call | tf_op jit(solution)/shard_map/gather_grids/pallas_call | solution.py:438
  55.2 0.0 copy-start
  55.2 1.3 %copy-done = f32[64,64,128]{2,1,0:T(8,128)} copy-done((f32[64,64,128]{2,1,0:T(8,128)}, f32[64,64,128]{2,1,0:T(8,128)S(1)}, u32[]{:S(2)}) %copy-start) | copy-done | bytes 2097176
  56.5 0.0 copy-start.3
  56.5 0.9 copy-done.3
  57.4 0.0 copy-start.4
  57.4 0.9 copy-done.4
  58.3 0.0 copy-start.5
  58.3 0.8 copy-done.5
  59.1 0.0 copy-start.6
  59.1 0.8 copy-done.6
  60.0 0.0 copy-start.7
  60.0 0.7 copy-done.7
  60.6 19.8 %apply_pair.1.partial = f32[64,64,128]{2,1,0:T(8,128)S(1)} custom-call(f32[8,3]{1,0:T(8,128)S(1)} %copy.10.shift_table, s32[4]{0:T(128)S(1)} %copy-done.7, f32[64,64,128]{2,1,0:T(8,128)S(1)} %get-tuple-element.7.orbital_grid, f32[64,64,128]{2,1,0:T(8,128)} %copy-done, bf16[256,256]{1,0:T(8,128)(2,1)S(1)} %copy-done.4, bf16[256,256]{1,0:T(8,128)(2,1)S(1)} %copy-done.3, ...), custom_call_target="tpu_custom_call" | custom-call | tf_op jit(solution)/shard_map/apply_pair/pallas_call | solution.py:922
  80.5 46.8 %finish.1 = (f32[16,64,128]{2,1,0:T(8,128)S(1)}, f32[16,64,128]{2,1,0:T(8,128)S(1)}) custom-call(f32[64,64,128]{2,1,0:T(8,128)S(1)} %apply_pair.1.partial, f32[4,4,64,128]{3,2,1,0:T(8,128)S(1)} %get-tuple-element.9.orbital_parts), custom_call_target="tpu_custom_call" | custom-call | tf_op jit(solution)/shard_map/finish/pallas_call | solution.py:738
  127.3 0.8 copy.13
  128.0 0.8 copy.14
Async XLA Ops:
  1.4 1.0 copy-start.1
  2.4 1.0 copy-start.2
  55.2 1.3 %copy-start = (f32[64,64,128]{2,1,0:T(8,128)}, f32[64,64,128]{2,1,0:T(8,128)S(1)}, u32[]{:S(2)}) copy-start(f32[64,64,128]{2,1,0:T(8,128)S(1)} %get-tuple-element.8.partner_grid) | copy-start | bytes 6291460
  56.5 0.9 copy-start.3
  57.4 0.9 copy-start.4
  58.3 0.8 copy-start.5
  59.1 0.8 copy-start.6
  60.0 0.7 copy-start.7

commit v3 on v0

--- a/solution.py
+++ b/solution.py
@@ -1,11 +1,18 @@
+import functools
 import math
 
 import jax
 import jax.numpy as jnp
+import numpy as np
 from jax import lax
+from jax.experimental import pallas as pl
+from jax.experimental.pallas import tpu as pltpu
 from jax.sharding import PartitionSpec as P
 
 HIGHEST = lax.Precision.HIGHEST
+HIGH = lax.Precision.HIGH
+MESH = pl.DeviceIdType.MESH
+GROUP = 8
 SCREEN_SQUARE = 0.25
 FOUR_PI = 4.0 * math.pi
 
@@ -32,7 +39,7 @@
 def along_last(field, table):
     shape = field.shape
     flat = field.reshape(-1, shape[-1])
-    return jnp.dot(flat, table, precision=HIGHEST).reshape(shape)
+    return jnp.dot(flat, table, precision=HIGH).reshape(shape)
 
 
 def along_axis(field, table, axis_number):
@@ -40,9 +47,9 @@
     extent = shape[-1] // 2
     split = field.reshape(shape[0], shape[1], shape[2], 2, extent)
     if axis_number == 1:
-        result = jnp.einsum("kcnd,pnbdz->pkbcz", table, split, precision=HIGHEST)
+        result = jnp.einsum("kcnd,pnbdz->pkbcz", table, split, precision=HIGH)
     else:
-        result = jnp.einsum("kcnd,pandz->pakcz", table, split, precision=HIGHEST)
+        result = jnp.einsum("kcnd,pandz->pakcz", table, split, precision=HIGH)
     return result.reshape(shape)
 
 
@@ -160,7 +167,7 @@
     return lax.fori_loop(0, matrix_order, solve_step, (zero_start, zero_start))
 
 
-def body(orbitals, partners, shift_table, shift_index):
+def general_body(orbitals, partners, shift_table, shift_index):
     extent = orbitals.shape[2]
     band_count = orbitals.shape[0]
     tables = (
@@ -220,6 +227,685 @@
     return (potential, projector.reshape(orbitals.shape))
 
 
+def remote(source, target, send_sem, recv_sem, where):
+    return pltpu.make_async_remote_copy(
+        src_ref=source,
+        dst_ref=target,
+        send_sem=send_sem,
+        recv_sem=recv_sem,
+        device_id=where,
+        device_id_type=MESH,
+    )
+
+
+def greet(others):
+    barrier = pltpu.get_barrier_semaphore()
+    for other in others:
+        pl.semaphore_signal(barrier, inc=1, device_id=other, device_id_type=MESH)
+    pl.semaphore_wait(barrier, len(others))
+
+
+def turn(block):
+    lanes = block.shape[-1]
+    swapped = pltpu.roll(block, lanes // 2, block.ndim - 1)
+    position = lax.broadcasted_iota(jnp.int32, block.shape, block.ndim - 1)
+    return jnp.where(position < lanes // 2, swapped, -swapped)
+
+
+def small_factor_inverse(matrix):
+    order = len(matrix)
+    lower = [[None] * order for _ in range(order)]
+    for column in range(order):
+        residual = []
+        for row in range(column, order):
+            real, imag = matrix[row][column]
+            for k in range(column):
+                a, b = lower[row][k]
+                c, d = lower[column][k]
+                real = real - (a * c + b * d)
+                imag = imag - (b * c - a * d)
+            residual.append((real, imag))
+        pivot = jnp.sqrt(residual[0][0])
+        lower[column][column] = (pivot, jnp.zeros_like(pivot))
+        for row in range(column + 1, order):
+            real, imag = residual[row - column]
+            lower[row][column] = (real / pivot, imag / pivot)
+    inverse = [[None] * order for _ in range(order)]
+    for row in range(order):
+        pivot = lower[row][row][0]
+        inverse[row][row] = (1.0 / pivot, jnp.zeros_like(pivot))
+        for column in range(row):
+            real = jnp.zeros_like(pivot)
+            imag = jnp.zeros_like(pivot)
+            for k in range(column, row):
+                a, b = lower[row][k]
+                c, d = inverse[k][column]
+                real = real - (a * c - b * d)
+                imag = imag - (a * d + b * c)
+            inverse[row][column] = (real / pivot, imag / pivot)
+    return inverse
+
+
+def split_table(table):
+    high = table.astype(jnp.bfloat16)
+    low = (table - high.astype(np.float64)).astype(jnp.bfloat16)
+    return high, low
+
+
+def right_table(extent, sign):
+    grid = np.outer(np.arange(extent), np.arange(extent)) % extent
+    angle = 2.0 * math.pi / extent * grid
+    cosine, sine = np.cos(angle), sign * np.sin(angle)
+    table = np.block([[cosine, sine], [-sine, cosine]])
+    high, low = split_table(table)
+    upper = np.concatenate([high, low], axis=1)
+    lower = np.concatenate([high, np.zeros_like(low)], axis=1)
+    return np.concatenate([upper, lower], axis=0)
+
+
+def left_table(extent, sign):
+    grid = np.outer(np.arange(extent), np.arange(extent)) % extent
+    angle = 2.0 * math.pi / extent * grid
+    high, low = split_table(np.concatenate([np.cos(angle), sign * np.sin(angle)], axis=0))
+    return np.concatenate([high, high, low], axis=1)
+
+
+def halves(value):
+    high = value.astype(jnp.bfloat16)
+    low = (value - high.astype(jnp.float32)).astype(jnp.bfloat16)
+    return high, low
+
+
+def right_product(value, table):
+    lanes = value.shape[-1]
+    high, low = halves(value)
+    both = jnp.dot(
+        jnp.concatenate([high, low], axis=1), table, preferred_element_type=jnp.float32
+    )
+    return both[:, :lanes] + both[:, lanes:]
+
+
+def left_product(first, second, table):
+    rows, lanes = first.shape
+    high, low = halves(jnp.concatenate([first, second], axis=1))
+    stacked = jnp.concatenate([high, low, high], axis=0)
+    both = jnp.dot(table, stacked, preferred_element_type=jnp.float32)
+    return tuple(
+        both[:rows, cut : cut + lanes] - turn(both[rows:, cut : cut + lanes])
+        for cut in (0, lanes)
+    )
+
+
+def spread_parts(value):
+    lanes = value.shape[-1]
+    swapped = pltpu.roll(value, lanes // 2, value.ndim - 1)
+    lower = lax.broadcasted_iota(jnp.int32, value.shape, value.ndim - 1) < lanes // 2
+    return jnp.where(lower, value, swapped), jnp.where(lower, swapped, value)
+
+
+def forward_group(group, orbital_grid, partner_grid, work, right, left):
+    rows, lanes = orbital_grid.shape[1:]
+    span = pl.ds(group * GROUP, GROUP)
+    orbital = orbital_grid[span].reshape(GROUP * rows, lanes)
+    real, imag = spread_parts(partner_grid[span].reshape(GROUP * rows, lanes))
+    density = real * orbital + imag * turn(orbital)
+    lines = right_product(density, right[...])
+    planes = []
+    for pair in range(GROUP // 2):
+        start = 2 * pair * rows
+        planes += left_product(
+            lines[start : start + rows], lines[start + rows : start + 2 * rows], left[...]
+        )
+    stacked = jnp.stack(planes, axis=0)
+    work[:, span, :] = jnp.swapaxes(stacked, 0, 1)
+
+
+def backward_group(group, partner_grid, partial, work, right, left):
+    rows, lanes = partner_grid.shape[1:]
+    span = pl.ds(group * GROUP, GROUP)
+    planes = jnp.swapaxes(work[:, span, :], 0, 1)
+    lines = []
+    for pair in range(GROUP // 2):
+        lines += left_product(planes[2 * pair], planes[2 * pair + 1], left[...])
+    field = right_product(jnp.concatenate(lines, axis=0), right[...])
+    real, imag = spread_parts(partner_grid[span].reshape(GROUP * rows, lanes))
+    partial[span] = (real * field - imag * turn(field)).reshape(GROUP, rows, lanes)
+
+
+def middle_pairs(shift, work, forward, inverse):
+    columns, extent, lanes = work.shape
+    first = frequency(lax.broadcasted_iota(jnp.int32, (extent, lanes), 0), extent)
+    third_place = lax.broadcasted_iota(jnp.int32, (extent, lanes), 1)
+    third_place = jnp.where(third_place < lanes // 2, third_place, third_place - lanes // 2)
+    third = frequency(third_place, extent)
+    base = (first + shift[0]) ** 2 + (third + shift[2]) ** 2 + SCREEN_SQUARE
+    scale = FOUR_PI / (float(extent) * float(columns) * float(lanes // 2))
+
+    def one_pair(pair, carry):
+        spectra = left_product(work[2 * pair], work[2 * pair + 1], forward[...])
+        scaled = []
+        for which in range(2):
+            column = 2 * pair + which
+            second = jnp.where(column < columns // 2, column, column - columns)
+            offset = (second.astype(jnp.float32) + shift[1]) ** 2
+            scaled.append(spectra[which] * (scale / (base + offset)))
+        fields = left_product(scaled[0], scaled[1], inverse[...])
+        work[2 * pair] = fields[0]
+        work[2 * pair + 1] = fields[1]
+        return carry
+
+    lax.fori_loop(0, columns // 2, one_pair, 0, unroll=2)
+
+
+def exchange_kernel(
+    bands,
+    ranks,
+    shift_table,
+    shift_index,
+    orbital,
+    partner,
+    right_forward,
+    right_inverse,
+    left_forward,
+    left_inverse,
+    potential,
+    projector,
+    orbital_grid,
+    partner_grid,
+    orbital_parts,
+    from_below,
+    from_above,
+    work,
+    partial,
+    near,
+    outgoing,
+    arriving,
+    potential_parts,
+    projector_parts,
+    own_sums,
+    all_sums,
+    chain_send,
+    chain_recv,
+    deliver_send,
+    deliver_recv,
+    grid_send,
+    grid_recv,
+    early_send,
+    early_recv,
+    local_sem,
+    near_send,
+    near_recv,
+    far_send,
+    far_recv,
+    part_send,
+    part_recv,
+    sum_send,
+    sum_recv,
+    back_send,
+    back_recv,
+):
+    band = lax.axis_index("band")
+    rank = lax.axis_index("fft")
+    planes, rows, lanes = orbital.shape
+    piece = planes // bands
+    per_group = GROUP // piece
+    halves_count = planes // GROUP
+    greet(
+        [
+            {"band": (band + step) % bands, "fft": (rank + turn_by) % ranks}
+            for step in range(bands)
+            for turn_by in range(ranks)
+            if step or turn_by
+        ]
+    )
+
+    def span(index):
+        return pl.ds(index * piece, piece)
+
+    def slab(index):
+        return pl.ds(index * planes, planes)
+
+    beside = rank + 1 - 2 * (rank % 2)
+    across = (rank + 2) % ranks
+    beside_across = (beside + 2) % ranks
+
+    def chain_copy(upward, distance, chunk):
+        held = from_below if upward else from_above
+        source = partner.at[span(chunk)] if distance == 0 else held.at[distance - 1, chunk]
+        way = 0 if upward else 1
+        return remote(
+            source,
+            held.at[distance, chunk],
+            chain_send.at[way, distance, chunk],
+            chain_recv.at[way, distance, chunk],
+            {"band": band + 1 if upward else band - 1},
+        )
+
+    def deliver(upward, distance, chunk, act):
+        held = from_below if upward else from_above
+        source = partner.at[span(chunk)] if distance == 0 else held.at[distance - 1, chunk]
+        owner = band - distance if upward else band + distance
+        target = partner_grid.at[pl.ds(rank * planes + chunk * piece, piece)]
+        way = 0 if upward else 1
+
+        @pl.when(owner == rank)
+        def _():
+            if act == "start":
+                pltpu.make_async_copy(source, target, local_sem.at[chunk]).start()
+
+        @pl.when(owner != rank)
+        def _():
+            copy = remote(
+                source,
+                target,
+                deliver_send.at[way, distance, chunk],
+                deliver_recv.at[rank, chunk],
+                {"fft": owner},
+            )
+            copy.start() if act == "start" else copy.wait_send()
+
+    def has_source(upward, distance):
+        return band >= distance if upward else band + distance <= bands - 1
+
+    def has_next(upward):
+        return band <= bands - 2 if upward else band >= 1
+
+    def both(first, second):
+        return jnp.logical_and(first, second)
+
+    def forward_half(half):
+        for chunk in range(half * per_group, (half + 1) * per_group):
+            target = partner_grid.at[pl.ds(rank * planes + chunk * piece, piece)]
+            pltpu.make_async_copy(partner.at[span(chunk)], target, local_sem.at[chunk]).wait()
+            for step in range(1, ranks):
+                source = (rank + step) % ranks
+                target = partner_grid.at[pl.ds(source * planes + chunk * piece, piece)]
+                remote(
+                    target,
+                    target,
+                    deliver_send.at[0, 0, chunk],
+                    deliver_recv.at[source, chunk],
+                    {"fft": source},
+                ).wait_recv()
+
+        def forward(index, carry):
+            forward_group(
+                index * halves_count + half,
+                orbital_grid,
+                partner_grid,
+                work,
+                right_forward,
+                left_forward,
+            )
+            return carry
+
+        lax.fori_loop(0, ranks, forward, 0)
+
+    for chunk in range(bands):
+        for upward in (True, False):
+
+            @pl.when(has_next(upward))
+            def _():
+                chain_copy(upward, 0, chunk).start()
+
+    to_across = remote(
+        orbital, orbital_grid.at[slab(rank)], grid_send.at[0], grid_recv.at[0], {"fft": across}
+    )
+    to_beside = remote(
+        orbital, orbital_grid.at[slab(rank)], grid_send.at[1], grid_recv.at[1], {"fft": beside}
+    )
+    to_across.start()
+    to_beside.start()
+    own_grid = pltpu.make_async_copy(orbital, orbital_grid.at[slab(rank)], local_sem.at[bands])
+    own_grid.start()
+    for chunk in range(bands):
+        deliver(True, 0, chunk, "start")
+    onward = remote(
+        orbital_grid.at[slab(across)],
+        orbital_grid.at[slab(across)],
+        grid_send.at[2],
+        grid_recv.at[2],
+        {"fft": beside},
+    )
+    for distance in range(1, bands):
+        for chunk in range(bands):
+            for upward in (True, False):
+
+                @pl.when(has_source(upward, distance))
+                def _():
+                    chain_copy(upward, distance - 1, chunk).wait_recv()
+
+                if distance < bands - 1:
+
+                    @pl.when(both(has_source(upward, distance), has_next(upward)))
+                    def _():
+                        chain_copy(upward, distance, chunk).start()
+
+                @pl.when(has_source(upward, distance))
+                def _():
+                    deliver(upward, distance, chunk, "start")
+
+            if distance == bands - 1 and chunk > 0 and chunk % per_group == 0:
+                forward_half(chunk // per_group - 1)
+
+        if distance == 1:
+            to_across.wait_recv()
+            onward.start()
+            own_grid.wait()
+            to_beside.wait_recv()
+            onward.wait_recv()
+    forward_half(halves_count - 1)
+    early_copies = []
+    for step in range(1, bands):
+        other = (band + step) % bands
+        copy = remote(
+            orbital.at[span(other)],
+            orbital_parts.at[band],
+            early_send.at[step - 1],
+            early_recv.at[step - 1],
+            {"band": other},
+        )
+        copy.start()
+        early_copies.append(copy)
+    own_part = pltpu.make_async_copy(
+        orbital.at[span(band)], orbital_parts.at[band], local_sem.at[bands + 1]
+    )
+    own_part.start()
+
+    chosen = shift_index[rank]
+    shift = [shift_table[chosen, axis] for axis in range(3)]
+    middle_pairs(shift, work, left_forward, left_inverse)
+
+    def backward_slab(index):
+        def backward(half, carry):
+            backward_group(
+                index * halves_count + half, partner_grid, partial, work, right_inverse, left_inverse
+            )
+            return carry
+
+        lax.fori_loop(0, halves_count, backward, 0)
+
+    def near_copy(which, index):
+        return remote(
+            partial.at[slab(index)],
+            near.at[which],
+            near_send.at[which],
+            near_recv.at[which],
+            {"fft": beside},
+        )
+
+    def far_copy(chunk):
+        return remote(
+            outgoing.at[chunk],
+            arriving.at[chunk],
+            far_send.at[chunk],
+            far_recv.at[chunk],
+            {"fft": across},
+        )
+
+    def window(index, chunk):
+        return pl.ds(index * planes + chunk * piece, piece)
+
+    turns = [(band + step) % bands for step in range(1, bands + 1)]
+    backward_slab(beside_across)
+    near_copy(1, beside_across).start()
+    backward_slab(across)
+    near_copy(1, beside_across).wait_recv()
+    for chunk in turns:
+        outgoing[chunk] = partial[window(across, chunk)] + near[1, span(chunk)]
+        far_copy(chunk).start()
+    backward_slab(beside)
+    near_copy(0, beside).start()
+    backward_slab(rank)
+    near_copy(0, beside).wait_recv()
+
+    def part_copy(chunk):
+        return remote(
+            potential.at[span(chunk)],
+            potential_parts.at[band],
+            part_send.at[chunk],
+            part_recv.at[band],
+            {"band": chunk},
+        )
+
+    for step, chunk in enumerate(turns):
+        far_copy(chunk).wait_recv()
+        potential[span(chunk)] = (
+            partial[window(rank, chunk)] + near[0, span(chunk)]
+        ) + arriving[chunk]
+        if step < bands - 1:
+            part_copy(chunk).start()
+        else:
+            potential_parts[band] = potential[span(band)]
+    for chunk in turns[:-1]:
+        remote(
+            potential_parts.at[chunk],
+            potential_parts.at[chunk],
+            part_send.at[chunk],
+            part_recv.at[chunk],
+            {"band": chunk},
+        ).wait_recv()
+    for copy in early_copies:
+        copy.wait()
+    own_part.wait()
+
+    entries = [(i, l) for i in range(bands) for l in range(i + 1)]
+    position = lax.broadcasted_iota(jnp.int32, (8, lanes), 1)
+
+    def accumulate(plane, sums):
+        turned = []
+        straight = []
+        for l in range(bands):
+            block = potential_parts[l, plane]
+            straight.append(block)
+            turned.append(turn(block))
+        result = []
+        for number, (i, l) in enumerate(entries):
+            left = orbital_parts[i, plane]
+            for half, right in enumerate((straight[l], turned[l])):
+                product = (left * right).reshape(rows // 8, 8, lanes)
+                result.append(sums[2 * number + half] + jnp.sum(product, axis=0))
+        return tuple(result)
+
+    zero = jnp.zeros((8, lanes), jnp.float32)
+    sums = lax.fori_loop(0, piece, accumulate, (zero,) * (2 * len(entries)))
+    packed = zero
+    for number, value in enumerate(sums):
+        packed = jnp.where(position == number, jnp.sum(value, axis=1, keepdims=True), packed)
+    own_sums[...] = packed
+    sum_copies = []
+    number = 0
+    for step in range(bands):
+        for turn_by in range(ranks):
+            if step == 0 and turn_by == 0:
+                continue
+            copy = remote(
+                own_sums,
+                all_sums.at[band, rank],
+                sum_send.at[step, turn_by],
+                sum_recv.at[step, turn_by],
+                {"band": (band + step) % bands, "fft": (rank + turn_by) % ranks},
+            )
+            copy.start()
+            sum_copies.append(copy)
+    all_sums[band, rank] = packed
+    for copy in sum_copies:
+        copy.wait()
+    total = zero
+    for one_band in range(bands):
+        for one_rank in range(ranks):
+            total = total + all_sums[one_band, one_rank]
+    total = jnp.broadcast_to(jnp.sum(total, axis=0, keepdims=True), (8, lanes))
+    volume = float(lanes // 2) * float(rows) * float(planes * ranks)
+    matrix = [[None] * bands for _ in range(bands)]
+    for number, (i, l) in enumerate(entries):
+        values = [
+            jnp.broadcast_to(
+                jnp.sum(jnp.where(position == 2 * number + half, total, 0.0), axis=1, keepdims=True),
+                (8, lanes),
+            )
+            / volume
+            for half in range(2)
+        ]
+        matrix[i][l] = (values[0], values[1])
+    inverse = small_factor_inverse(matrix)
+    back_copies = []
+
+    def spread(value):
+        return value[:1]
+
+    for l in range(bands):
+
+        def combine(plane, carry):
+            sum_straight = jnp.zeros((rows, lanes), jnp.float32)
+            sum_turned = jnp.zeros((rows, lanes), jnp.float32)
+            for m in range(l + 1):
+                block = potential_parts[m, plane]
+                real, imag = inverse[l][m]
+                sum_straight = sum_straight + spread(real) * block
+                sum_turned = sum_turned + spread(imag) * block
+            projector_parts[l, plane] = sum_straight + turn(sum_turned)
+            return carry
+
+        lax.fori_loop(0, piece, combine, 0)
+
+    for chunk in turns[1:-1] + turns[:1]:
+        remote(
+            projector_parts.at[chunk],
+            projector.at[span(band)],
+            back_send.at[chunk],
+            back_recv.at[band],
+            {"band": chunk},
+        ).start()
+    projector[span(band)] = projector_parts[band]
+    for chunk in turns[:-1]:
+        back = remote(
+            projector_parts.at[chunk],
+            projector.at[span(chunk)],
+            back_send.at[chunk],
+            back_recv.at[chunk],
+            {"band": chunk},
+        )
+        back.wait_recv()
+        back.wait_send()
+        part_copy(chunk).wait_send()
+    for chunk in turns:
+        far_copy(chunk).wait_send()
+    near_copy(0, beside).wait_send()
+    near_copy(1, beside_across).wait_send()
+    to_across.wait_send()
+    to_beside.wait_send()
+    onward.wait_send()
+    for distance in range(bands):
+        for chunk in range(bands):
+            for upward in (True, False):
+                if distance < bands - 1:
+
+                    @pl.when(both(has_source(upward, distance), has_next(upward)))
+                    def _():
+                        chain_copy(upward, distance, chunk).wait_send()
+
+                if distance > 0 or upward:
+
+                    @pl.when(has_source(upward, distance))
+                    def _():
+                        deliver(upward, distance, chunk, "wait")
+
+
+def exchange(bands, ranks, orbital, partner, shift_table, shift_index):
+    planes, rows, lanes = orbital.shape
+    piece = planes // bands
+    vmem = pl.BlockSpec(memory_space=pltpu.VMEM)
+    smem = pl.BlockSpec(memory_space=pltpu.SMEM)
+    out = jax.ShapeDtypeStruct((planes, rows, lanes), jnp.float32)
+    grid = pltpu.VMEM((ranks * planes, rows, lanes), jnp.float32)
+    held = pltpu.VMEM((bands - 1, bands, piece, rows, lanes), jnp.float32)
+    quarters = pltpu.VMEM((bands, piece, rows, lanes), jnp.float32)
+    dma = pltpu.SemaphoreType.DMA
+    tables = [
+        jnp.asarray(table)
+        for table in (
+            right_table(rows, -1.0),
+            right_table(rows, 1.0),
+            left_table(rows, -1.0),
+            left_table(rows, 1.0),
+        )
+    ]
+    return pl.pallas_call(
+        functools.partial(exchange_kernel, bands, ranks),
+        name="exchange",
+        out_shape=(out, out),
+        in_specs=[smem, smem] + [vmem] * 6,
+        out_specs=(vmem, vmem),
+        scratch_shapes=[
+            grid,
+            grid,
+            quarters,
+            held,
+            held,
+            grid,
+            grid,
+            pltpu.VMEM((2, planes, rows, lanes), jnp.float32),
+            quarters,
+            quarters,
+            quarters,
+            quarters,
+            pltpu.VMEM((8, lanes), jnp.float32),
+            pltpu.VMEM((bands, ranks, 8, lanes), jnp.float32),
+            dma((2, bands, bands)),
+            dma((2, bands, bands)),
+            dma((2, bands, bands)),
+            dma((ranks, bands)),
+            dma((3,)),
+            dma((3,)),
+            dma((bands,)),
+            dma((bands,)),
+            dma((bands + 2,)),
+            dma((2,)),
+            dma((2,)),
+            dma((bands,)),
+            dma((bands,)),
+            dma((bands,)),
+            dma((bands,)),
+            dma((bands, ranks)),
+            dma((bands, ranks)),
+            dma((bands,)),
+            dma((bands,)),
+        ],
+        compiler_params=pltpu.CompilerParams(
+            collective_id=0, has_side_effects=True, vmem_limit_bytes=48 * 1024 * 1024
+        ),
+    )(shift_table, shift_index, orbital, partner, *tables)
+
+
+def paired_body(bands, ranks, orbitals, partners, shift_table, shift_index):
+    potential, projector = exchange(
+        bands, ranks, orbitals[0], partners[0], shift_table, shift_index
+    )
+    return (potential[None], projector[None])
+
+
+def body(orbitals, partners, shift_table, shift_index):
+    bands = lax.axis_size("band")
+    ranks = lax.axis_size("fft")
+    count, planes, rows, lanes = orbitals.shape
+    grid_bytes = ranks * planes * rows * lanes * 4
+    paired = (
+        count == 1
+        and ranks == 4
+        and bands == ranks
+        and planes % bands == 0
+        and planes % GROUP == 0
+        and GROUP % (planes // bands) == 0
+        and lanes == 2 * rows
+        and lanes == 128
+        and grid_bytes <= 2 * 1024 * 1024
+    )
+    if paired:
+        return paired_body(bands, ranks, orbitals, partners, shift_table, shift_index)
+    return general_body(orbitals, partners, shift_table, shift_index)
+
+
 def solution(mesh):
     in_specs = (
         P(("kgrp", "band"), "fft", None, None),

time: 325 us -> 105 us (0.32); the launches traced: 319 us -> 104 us
  waiting for transfers between devices: 159 us -> 0 us
  Pallas kernels: 0 us -> 95.1 us
  matrix products: 81.9 us -> 0 us
  blocking collectives: 23.5 us -> 0 us
  between operations: 14.4 us -> 0.65 us
  other arithmetic: 12.9 us -> 0 us
  local copies, waits for them, and re-layouts: 20.2 us -> 8.48 us
  starting transfers between devices: 3.98 us -> 0 us
    all_gather x3 -> x0, waiting for transfers between devices: 123 us -> none  [the longest x1 49.1 us: body(): every_slab = lax.all_gather(partners, 'band', axis=0, tiled=True)]
    pallas_call x0 -> x1, Pallas kernels: none -> 95.1 us  [exchange(): pl.pallas_call(functools.partial(exchange_kernel, bands, ranks), name='ex...]
    dot_general x43 -> x0, matrix products: 81.9 us -> none  [the longest x2 13.3 us: along_last(): return jnp.dot(flat, table, precision=HIGHEST).reshape(shape)]
    reduce_scatter x1 -> x0, waiting for transfers between devices: 28.9 us -> none  [body(): lax.psum_scatter(partial_value, 'fft', scatter_dimension=1, tiled=True)]
    all_gather x2 -> x0, blocking collectives: 17.1 us -> none  [the longest x1 9.15 us: body(): lax.all_gather(summed_real, 'band', axis=0, tiled=True)]
    another operation x2 -> x0, local copies, waits for them, and re-layouts: 12.2 us -> none
    unnamed x14 -> x19, local copies, waits for them, and re-layouts: 1.56 us -> 8.48 us
    psum x1 -> x0, blocking collectives: 6.38 us -> none  [body(): summed_real, summed_imag = lax.psum((rows_real, rows_imag), 'fft')]
  transfers between devices with their start and end apart: 5 -> 0, of which waited for: 5 -> 0; matrix products, arithmetic and copies ran while one was open for 2% -> 0% of each run, Pallas kernels for 0% -> 0%
where the time goes in v3:
time: 105 us; the launch traced here: 104 us
  Pallas kernels  95.1 us (91%)
  local copies, waits for them, and re-layouts  8.48 us (8%)
    pallas_call x1, Pallas kernels, exchange(): pl.pallas_call(functools.partial(exchange_kernel, bands, ranks), name='ex...  95.1 us
    unnamed x19, local copies, waits for them, and re-layouts  8.48 us

profile of v3, /device:TPU:0, one launch (start us, length us, event | category | flops | bytes accessed | tf_op | source)
XLA Modules:
  0.0 104.2 jit_solution(9153660448185302120)
XLA Ops:
  0.6 0.0 copy-start.7
  0.6 0.7 copy-done.7
  1.3 0.0 copy-start.6
  1.3 0.1 copy.10.shift_table
  1.4 0.6 copy-done.6
  2.0 0.0 copy-start
  2.0 1.0 copy-done
  3.0 0.0 copy-start.1
  3.0 1.0 copy-done.1
  4.1 0.0 copy-start.2
  4.1 0.9 copy-done.2
  5.0 0.0 copy-start.3
  5.0 0.9 copy-done.3
  5.9 0.0 copy-start.4
  5.9 0.8 copy-done.4
  6.7 0.0 copy-start.5
  6.7 0.8 copy-done.5
  7.5 95.1 %exchange.1 = (f32[16,64,128]{2,1,0:T(8,128)S(1)}, f32[16,64,128]{2,1,0:T(8,128)S(1)}) custom-call(f32[8,3]{1,0:T(8,128)S(1)} %copy.10.shift_table, s32[4]{0:T(128)S(1)} %copy-done.6, f32[16,64,128]{2,1,0:T(8,128)S(1)} %bitcast.4, f32[16,64,128]{2,1,0:T(8,128)S(1)} %bitcast.5, bf16[256,256]{1,0:T(8,128)(2,1)S(1)} %copy-done.3, ...), custom_call_target="tpu_custom_call" | custom-call | tf_op jit(solution)/shard_map/exchange/pallas_call | solution.py:834
  102.6 0.8 copy.13
  103.4 0.8 copy.14
Async XLA Ops:
  0.6 0.7 copy-start.7
  1.3 0.7 copy-start.6
  2.0 1.0 copy-start
  3.0 1.0 copy-start.1
  4.1 0.9 copy-start.2
  5.0 0.9 copy-start.3
  5.9 0.8 copy-start.4
  6.7 0.8 copy-start.5

commit v4 on v3

--- a/solution.py
+++ b/solution.py
@@ -394,7 +394,7 @@
         work[2 * pair + 1] = fields[1]
         return carry
 
-    lax.fori_loop(0, columns // 2, one_pair, 0, unroll=2)
+    lax.fori_loop(0, columns // 2, one_pair, 0, unroll=4)
 
 
 def exchange_kernel(
@@ -402,12 +402,12 @@
     ranks,
     shift_table,
     shift_index,
-    orbital,
-    partner,
-    right_forward,
-    right_inverse,
-    left_forward,
-    left_inverse,
+    orbital_home,
+    partner_home,
+    right_forward_home,
+    right_inverse_home,
+    left_forward_home,
+    left_inverse_home,
     potential,
     projector,
     orbital_grid,
@@ -443,7 +443,29 @@
     sum_recv,
     back_send,
     back_recv,
+    orbital,
+    partner,
+    right_forward,
+    right_inverse,
+    left_forward,
+    left_inverse,
+    load_sem,
 ):
+    loads = [
+        pltpu.make_async_copy(home, here, load_sem.at[number])
+        for number, (home, here) in enumerate(
+            (
+                (partner_home, partner),
+                (orbital_home, orbital),
+                (right_forward_home, right_forward),
+                (left_forward_home, left_forward),
+                (right_inverse_home, right_inverse),
+                (left_inverse_home, left_inverse),
+            )
+        )
+    ]
+    for load in loads:
+        load.start()
     band = lax.axis_index("band")
     rank = lax.axis_index("fft")
     planes, rows, lanes = orbital.shape
@@ -458,6 +480,7 @@
             if step or turn_by
         ]
     )
+    loads[0].wait()
 
     def span(index):
         return pl.ds(index * piece, piece)
@@ -548,6 +571,7 @@
             def _():
                 chain_copy(upward, 0, chunk).start()
 
+    loads[1].wait()
     to_across = remote(
         orbital, orbital_grid.at[slab(rank)], grid_send.at[0], grid_recv.at[0], {"fft": across}
     )
@@ -592,6 +616,8 @@
             to_across.wait_recv()
             onward.start()
             own_grid.wait()
+            for load in loads[2:]:
+                load.wait()
             to_beside.wait_recv()
             onward.wait_recv()
     forward_half(halves_count - 1)
@@ -835,7 +861,7 @@
         functools.partial(exchange_kernel, bands, ranks),
         name="exchange",
         out_shape=(out, out),
-        in_specs=[smem, smem] + [vmem] * 6,
+        in_specs=[smem, smem] + [pl.BlockSpec(memory_space=pl.ANY)] * 6,
         out_specs=(vmem, vmem),
         scratch_shapes=[
             grid,
@@ -871,9 +897,13 @@
             dma((bands, ranks)),
             dma((bands,)),
             dma((bands,)),
-        ],
+            pltpu.VMEM(orbital.shape, jnp.float32),
+            pltpu.VMEM(orbital.shape, jnp.float32),
+        ]
+        + [pltpu.VMEM(table.shape, table.dtype) for table in tables]
+        + [dma((6,))],
         compiler_params=pltpu.CompilerParams(
-            collective_id=0, has_side_effects=True, vmem_limit_bytes=48 * 1024 * 1024
+            collective_id=0, has_side_effects=True, vmem_limit_bytes=60 * 1024 * 1024
         ),
     )(shift_table, shift_index, orbital, partner, *tables)
 

time: 105 us -> 97.9 us (0.932)
  local copies, waits for them, and re-layouts: 8.48 us -> 4.09 us
  Pallas kernels: 95.1 us -> 92.6 us
    unnamed x19 -> x7, local copies, waits for them, and re-layouts: 8.48 us -> 4.09 us
    pallas_call x1, Pallas kernels: 95.1 us -> 92.6 us  [exchange(): pl.pallas_call(functools.partial(exchange_kernel, bands, ranks), name='ex...]
where the time goes in v4:
time: 97.9 us; the launch traced here: 97.3 us
  Pallas kernels  92.6 us (95%)
  local copies, waits for them, and re-layouts  4.09 us (4%)
    pallas_call x1, Pallas kernels, exchange(): pl.pallas_call(functools.partial(exchange_kernel, bands, ranks), name='ex...  92.6 us
    unnamed x7, local copies, waits for them, and re-layouts  4.09 us

profile of v4, /device:TPU:0, one launch (start us, length us, event | category | flops | bytes accessed | tf_op | source)
XLA Modules:
  0.0 97.3 jit_solution(8624981783102014120)
XLA Ops:
  0.6 0.0 copy-start.1
  0.6 0.7 copy-done.1
  1.3 0.7 copy.10.shift_table
  2.0 92.6 %exchange.1 = (f32[16,64,128]{2,1,0:T(8,128)}, f32[16,64,128]{2,1,0:T(8,128)}) custom-call(f32[8,3]{1,0:T(8,128)} %copy.10.shift_table, s32[4]{0:T(128)} %shift_index.1, f32[16,64,128]{2,1,0:T(8,128)} %bitcast.4, f32[16,64,128]{2,1,0:T(8,128)} %bitcast.5, bf16[256,256]{1,0:T(8,128)(2,1)} %constant.8.clone.right_forward_home, ...), custom_call_target="tpu_custom_call" | custom-call | tf_op jit(solution)/shard_map/exchange/pallas_call | solution.py:860
  94.5 0.0 copy-start
  94.6 1.9 %copy.13 = f32[1,16,64,128]{3,2,1,0:T(8,128)} copy(f32[1,16,64,128]{3,2,1,0:T(8,128)} %bitcast.7) | data formatting | bytes 1048576
  96.5 0.0 copy-done
  96.5 0.8 copy.14
Async XLA Ops:
  0.6 0.7 copy-start.1
  94.5 2.0 %copy-start = (f32[16,64,128]{2,1,0:T(8,128)S(1)}, f32[16,64,128]{2,1,0:T(8,128)}, u32[]{:S(2)}) copy-start(f32[16,64,128]{2,1,0:T(8,128)} %get-tuple-element.5) | copy-start | bytes 1572868
